TPU v7x, 128 devices: a whole 4x4x4 slice. The times are simulated.
128 devices in a mesh: row: 8 (over y_hi, z), col: 16 (over x, y_lo, core).
Axes of the slice: x: 4, y: 4 (y_hi: 2, y_lo: 2; y = y_hi * 2 + y_lo), z: 4, core: 2. Of those that a mesh axis runs over, the one named last changes fastest.
Arguments:
- region: float32 [8, 1024, 8, 1024], P(None, 'col', None, 'row'), may hold values from -6 to 6
- l_panels: bfloat16 [3, 1024, 11, 1024], P(None, 'col', None, 'row'), may hold values from -0.0625 to 0.0625
- u_panels: bfloat16 [3, 11, 1024, 1024], P(None, None, 'col', 'row'), may hold values from -0.0625 to 0.0625
- diag_inv: float32 [3, 1024, 1024], P(None, 'col', 'row'), may hold values from -6 to 6
- pattern: int32 [3, 11, 8], replicated, may hold values from 0 to 1, as said below
Outputs:
- inverse: float32 [11, 1024, 11, 1024], P(None, 'col', None, 'row')
Inputs may be any that keep to these rules, and one draw needn't show every extreme that they name: pattern[s] marks the 128-row blocks in the structure of supernode s: only blocks of segments after s; for the last supernode only blocks of the ancestor region; for every other supernode all blocks of one later supernode (its parent in the elimination tree) and otherwise only blocks that the parent's pattern also marks.
All inputs are finite; a program needn't handle non-finite values.
Results may differ from a plain program's by a relative error of at most 0.0003.
Values may be sent and summed in bfloat16 or wider, within the bound.
A program may use at most 128 MiB of HBM per device.

v0:
```python
import jax
import jax.numpy as jnp
from jax import lax
from jax.sharding import Mesh
from jax.sharding import PartitionSpec as P

BLK = 128
NSUP = 3
NSEG = 11
COL = ("col_0", "col_1", "col_2")


def in_order(tiles, dim):
    dims = list(tiles.shape[1:])
    dims[dim] *= tiles.shape[0]
    return jnp.moveaxis(tiles, 0, dim).reshape(dims)


def stacked_from(value, axes, sequence):
    tiles = value
    for k in sequence:
        tiles = lax.all_gather(tiles, axes[k])
    done = sequence[::-1]
    back = [done.index(k) for k in range(len(axes))]
    tiles = tiles.transpose(*back, *range(len(axes), tiles.ndim))
    return tiles.reshape(-1, *value.shape)


def whole_of(value, axes, sequence, dim):
    return in_order(stacked_from(value, axes, sequence), dim)


def from_everyone(value, axis):
    copies = jnp.broadcast_to(value, (lax.axis_size(axis), *value.shape))
    return lax.all_to_all(copies, axis, split_axis=0, concat_axis=0, tiled=True)


def gathered_copies(value, axis, dim):
    tiles = from_everyone(value, axis)
    return in_order(tiles, dim)


def in_blocks(value, dim, count):
    before, after = (value.shape[:dim], value.shape[dim + 1 :])
    return jnp.moveaxis(value.reshape(*before, count, -1, *after), dim, 0)


def summed_on_arrival(value, axis, dim):
    tiles = in_blocks(value, dim, lax.axis_size(axis))
    arrived = lax.all_to_all(tiles, axis, split_axis=0, concat_axis=0, tiled=True)
    return arrived.sum(axis=0)


def per_device(region, l_panels, u_panels, diag_inv, pattern):
    rows_here = region.shape[1]
    cols_here = region.shape[3]
    row_index = lax.axis_index("row")
    col_index = lax.axis_index(COL)
    block_mask = jnp.repeat(pattern.astype(jnp.float32), BLK, axis=2)
    mask_rows = lax.dynamic_slice_in_dim(block_mask, col_index * rows_here, rows_here, 2)
    mask_cols = lax.dynamic_slice_in_dim(block_mask, row_index * cols_here, cols_here, 2)
    inverse = jnp.zeros((NSEG, rows_here, NSEG, cols_here), jnp.float32)
    inverse = inverse.at[NSUP:, :, NSUP:, :].set(region)
    for level in reversed(range(NSUP)):
        start_seg = level + 1
        lower = l_panels[level][:, start_seg:, :] * mask_cols[level, None, start_seg:, :].astype(
            jnp.bfloat16
        )
        lower_full = whole_of(lower, COL, (1, 0, 2), 0).astype(jnp.float32)
        upper = u_panels[level][start_seg:] * mask_rows[level, start_seg:, :, None].astype(
            jnp.bfloat16
        )
        upper_full = gathered_copies(upper, "row", 2).astype(jnp.float32)
        known = inverse[start_seg:, :, start_seg:, :]
        col_terms = jnp.einsum("ajbk,wbk->ajw", known, lower_full, precision=lax.Precision.HIGHEST)
        col_sum = summed_on_arrival(col_terms, "row", 2)
        column = -mask_rows[level, start_seg:, :, None] * col_sum
        row_terms = jnp.einsum("akw,akbj->wbj", upper_full, known, precision=lax.Precision.HIGHEST)
        row_sum = lax.psum_scatter(row_terms, COL, scatter_dimension=0, tiled=True)
        row_panel = -mask_cols[level, None, start_seg:, :] * row_sum
        diag_terms = jnp.einsum(
            "wbj,vbj->wv", row_panel, lower_full, precision=lax.Precision.HIGHEST
        )
        diag_sum = summed_on_arrival(diag_terms, "row", 1)
        diagonal = diag_inv[level] - diag_sum
        inverse = inverse.at[start_seg:, :, level, :].set(column)
        inverse = inverse.at[level, :, start_seg:, :].set(row_panel)
        inverse = inverse.at[level, :, level, :].set(diagonal)
    return inverse


def solution(mesh):
    split = Mesh(
        mesh.devices.reshape(mesh.shape["row"], 4, 2, 2), ("row", "col_0", "col_1", "col_2")
    )
    in_specs = (
        P(None, COL, None, "row"),
        P(None, COL, None, "row"),
        P(None, None, COL, "row"),
        P(None, COL, "row"),
        P(),
    )
    out_specs = P(None, COL, None, "row")
    return jax.shard_map(
        per_device, mesh=split, in_specs=in_specs, out_specs=out_specs, check_vma=False
    )
```

profile of v0, /device:TPU:0, one launch (start us, length us, event | category | flops | bytes accessed | tf_op | source)
XLA Modules:
  0.0 451.6 jit_solution(8277220506679213530)
XLA Ops:
  9.6 5.8 %all-gather = bf16[128,8,128]{2,0,1:T(8,128)(2,1)S(1)} all-gather(bf16[64,8,128]{2,0,1:T(8,128)(2,1)S(1)} %slice_multiply_fusion.2), channel_id=2, replica_groups=mesh['row'=8,'col_0'=4,'col_1'=2,'col_2'=2] {'col_1'}, dimensions={0}, use_global_device_ids=true | all-gather | bytes 393216 | tf_op jit(solution)/shard_map/all_gather | solution.py:22
  16.5 5.8 %all-gather.3 = bf16[128,9,128]{2,0,1:T(8,128)(2,1)S(1)} all-gather(bf16[64,9,128]{2,0,1:T(8,128)(2,1)S(1)} %slice_multiply_fusion.1), channel_id=5, replica_groups=mesh['row'=8,'col_0'=4,'col_1'=2,'col_2'=2] {'col_1'}, dimensions={0}, use_global_device_ids=true | all-gather | bytes 442368 | tf_op jit(solution)/shard_map/all_gather | solution.py:22
  23.2 20.0 %all-gather.16.cloned.1.call-done = bf16[8,64,8,128]{3,2,1,0:T(8,128)(2,1)} async-done(((bf16[2,64,8,128]{3,2,1,0:T(8,128)(2,1)}), bf16[8,64,8,128]{3,2,1,0:T(8,128)(2,1)}) %all-gather.16.cloned.1.call-update) | async-done | bytes 1048592 | tf_op jit(solution)/shard_map/all_gather | solution.py:22
  44.6 21.7 %all_to_all.45 = bf16[8,8,64,128]{3,2,1,0:T(8,128)(2,1)S(1)} all-to-all(bf16[8,8,64,128]{3,2,1,0:T(8,128)(2,1)S(1)} %broadcast_in_dim.14), channel_id=1, replica_groups=mesh['row'=8,'col_0'=4,'col_1'=2,'col_2'=2] {'row'}, dimensions={0} | all-to-all | bytes 2097152 | tf_op jit(solution)/shard_map/all_to_all | solution.py:35
  68.3 6.4 %convolution_bitcast_fusion = f32[1024,8,128]{2,0,1:T(8,128)} fusion(bf16[8,64,1024,1]{2,1,0,3:T(8,128)(2,1)} %reshape.535, f32[8,64,8,128]{3,2,1,0:T(8,128)S(1)} %copy-done.2), kind=kOutput, calls=%fused_computation.12 | convolution fusion | flops 6442450944 | bytes 7340032 | tf_op jit(solution)/shard_map/akw,akbj->wbj/dot_general | solution.py:78
  87.3 6.2 %fusion.25 = f32[8,8,64,128]{3,2,1,0:T(8,128)} fusion(bf16[8,128,8,128,1]{3,1,2,4,0:T(8,128)(2,1)S(1)} %bitcast.212, f32[8,64,8,128]{3,2,1,0:T(8,128)} %param.25), kind=kOutput, calls=%fused_computation.18 | convolution fusion | flops 6442450944 | bytes 6291456 | tf_op jit(solution)/shard_map/ajbk,wbk->ajw/dot_general | solution.py:75
  93.4 16.1 %all-to-all-done.4 = bf16[8,9,64,128]{3,2,1,0:T(8,128)(2,1)S(1)} async-done(((bf16[8,9,64,128]{3,2,1,0:T(8,128)(2,1)}), bf16[8,9,64,128]{3,2,1,0:T(8,128)(2,1)S(1)}, u32[]{:S(2)}, u32[]{:S(2)}) %all-to-all-start.4) | async-done | bytes 1179680 | tf_op jit(solution)/shard_map/all_to_all | solution.py:35
  109.5 4.5 %all-to-all-start = ((f32[8,8,64,128]{3,2,1,0:T(8,128)}), f32[8,8,64,128]{3,2,1,0:T(8,128)}, u32[]{:S(2)}, u32[]{:S(2)}) async-start(f32[8,8,64,128]{3,2,1,0:T(8,128)} %fusion.25), calls=%async_computation | async-start | bytes 4194304 | tf_op jit(solution)/shard_map/all_to_all | solution.py:50
  114.8 46.2 %all-gather.6 = bf16[128,10,128]{2,0,1:T(8,128)(2,1)S(1)} all-gather(bf16[64,10,128]{2,0,1:T(8,128)(2,1)S(1)} %slice_multiply_fusion), channel_id=8, replica_groups=mesh['row'=8,'col_0'=4,'col_1'=2,'col_2'=2] {'col_1'}, dimensions={0}, use_global_device_ids=true | all-gather | bytes 491520 | tf_op jit(solution)/shard_map/all_gather | solution.py:22
  178.3 6.8 %all-to-all-start.2 = ((f32[8,64,128]{2,1,0:T(8,128)}), f32[8,64,128]{2,1,0:T(8,128)S(1)}, u32[]{:S(2)}, u32[]{:S(2)}) async-start(f32[8,64,128]{2,1,0:T(8,128)} %convolution_bitcast_fusion.3), calls=%async_computation.3 | async-start | bytes 524288 | tf_op jit(solution)/shard_map/all_to_all | solution.py:50
  186.1 7.8 %all-to-all-done.2 = f32[8,64,128]{2,1,0:T(8,128)S(1)} async-done(((f32[8,64,128]{2,1,0:T(8,128)}), f32[8,64,128]{2,1,0:T(8,128)S(1)}, u32[]{:S(2)}, u32[]{:S(2)}) %all-to-all-start.2) | async-done | bytes 262176 | tf_op jit(solution)/shard_map/all_to_all | solution.py:50
  195.2 9.7 %fusion.13 = f32[1024,9,128]{2,0,1:T(8,128)} fusion(f32[11,64,11,128]{3,1,2,0:T(8,128)} %fusion.45, bf16[9,64,1024,1]{2,1,0,3:T(8,128)(2,1)S(1)} %reshape.542), kind=kOutput, calls=%fused_computation.11 | convolution fusion | flops 8153726976 | bytes 8552448 | tf_op jit(solution)/shard_map/akw,akbj->wbj/dot_general | solution.py:78
  215.4 4.8 %fusion.22 = f32[8,9,64,128]{3,2,0,1:T(8,128)S(1)} fusion(bf16[8,128,9,128,1]{3,1,2,0,4:T(8,128)(2,1)S(1)} %bitcast.210, f32[11,64,11,128]{3,1,2,0:T(8,128)S(1)} %copy-done), kind=kOutput, calls=%fused_computation.17 | convolution fusion | flops 8153726976 | bytes 7372800 | tf_op jit(solution)/shard_map/ajbk,wbk->ajw/dot_general | solution.py:75
  221.8 20.1 %all-to-all-done.7 = bf16[8,10,64,128]{3,2,1,0:T(8,128)(2,1)} async-done(((bf16[8,10,64,128]{3,2,1,0:T(8,128)(2,1)}), bf16[8,10,64,128]{3,2,1,0:T(8,128)(2,1)}, u32[]{:S(2)}, u32[]{:S(2)}) %all-to-all-start.7) | async-done | bytes 1310752 | tf_op jit(solution)/shard_map/all_to_all | solution.py:35
  241.9 5.0 %all-to-all-start.3 = ((f32[8,9,64,128]{3,2,1,0:T(8,128)}), f32[8,9,64,128]{3,2,1,0:T(8,128)}, u32[]{:S(2)}, u32[]{:S(2)}) async-start(f32[8,9,64,128]{3,2,1,0:T(8,128)} %copy.60), calls=%async_computation.4 | async-start | bytes 4718592 | tf_op jit(solution)/shard_map/all_to_all | solution.py:50
  255.8 42.6 %all-to-all-done.3 = f32[8,9,64,128]{3,2,1,0:T(8,128)} async-done(((f32[8,9,64,128]{3,2,1,0:T(8,128)}), f32[8,9,64,128]{3,2,1,0:T(8,128)}, u32[]{:S(2)}, u32[]{:S(2)}) %all-to-all-start.3) | async-done | bytes 2359328 | tf_op jit(solution)/shard_map/all_to_all | solution.py:50
  310.2 7.7 %all-to-all-done.5 = f32[8,64,128]{2,1,0:T(8,128)S(1)} async-done(((f32[8,64,128]{2,1,0:T(8,128)}), f32[8,64,128]{2,1,0:T(8,128)S(1)}, u32[]{:S(2)}, u32[]{:S(2)}) %all-to-all-start.5) | async-done | bytes 262176 | tf_op jit(solution)/shard_map/all_to_all | solution.py:50
  318.5 10.5 %fusion.10 = f32[1024,10,128]{2,0,1:T(8,128)} fusion(f32[11,64,11,128]{3,1,2,0:T(8,128)} %fusion.44, bf16[10,64,1024,1]{2,1,0,3:T(8,128)(2,1)} %reshape.549), kind=kOutput, calls=%fused_computation.10 | convolution fusion | flops 10066329600 | bytes 9830400 | tf_op jit(solution)/shard_map/akw,akbj->wbj/dot_general | solution.py:78
  332.0 5.3 %fusion.19 = f32[8,10,64,128]{3,2,0,1:T(8,128)S(1)} fusion(bf16[8,128,10,128,1]{3,1,2,0,4:T(8,128)(2,1)S(1)} %bitcast.208, f32[11,64,11,128]{3,1,2,0:T(8,128)S(1)} %copy-done.1), kind=kOutput, calls=%fused_computation.16 | convolution fusion | flops 10066329600 | bytes 8519680 | tf_op jit(solution)/shard_map/ajbk,wbk->ajw/dot_general | solution.py:75
  339.2 4.5 %all-to-all-start.6 = ((f32[8,10,64,128]{3,2,1,0:T(8,128)}), f32[8,10,64,128]{3,2,1,0:T(8,128)}, u32[]{:S(2)}, u32[]{:S(2)}) async-start(f32[8,10,64,128]{3,2,1,0:T(8,128)} %copy.65), calls=%async_computation.8 | async-start | bytes 5242880 | tf_op jit(solution)/shard_map/all_to_all | solution.py:50
  347.2 57.0 %all-to-all-done.6 = f32[8,10,64,128]{3,2,1,0:T(8,128)} async-done(((f32[8,10,64,128]{3,2,1,0:T(8,128)}), f32[8,10,64,128]{3,2,1,0:T(8,128)}, u32[]{:S(2)}, u32[]{:S(2)}) %all-to-all-start.6) | async-done | bytes 2621472 | tf_op jit(solution)/shard_map/all_to_all | solution.py:50
  407.1 17.1 %reduce-scatter.8.cloned.1.call-done = f32[64,10,128]{2,0,1:T(8,128)} async-done(((f32[1024,10,128]{2,0,1:T(8,128)}), f32[64,10,128]{2,0,1:T(8,128)}) %reduce-scatter.8.cloned.1.call-update) | async-done | bytes 327696 | tf_op jit(solution)/shard_map/reduce_scatter | solution.py:79
  428.4 6.3 %all-to-all-start.8 = ((f32[8,64,128]{2,1,0:T(8,128)}), f32[8,64,128]{2,1,0:T(8,128)S(1)}, u32[]{:S(2)}, u32[]{:S(2)}) async-start(f32[8,64,128]{2,1,0:T(8,128)} %convolution_bitcast_fusion.1), calls=%async_computation.11 | async-start | bytes 524288 | tf_op jit(solution)/shard_map/all_to_all | solution.py:50
  437.6 5.8 %all-to-all-done.8 = f32[8,64,128]{2,1,0:T(8,128)S(1)} async-done(((f32[8,64,128]{2,1,0:T(8,128)}), f32[8,64,128]{2,1,0:T(8,128)S(1)}, u32[]{:S(2)}, u32[]{:S(2)}) %all-to-all-start.8) | async-done | bytes 262176 | tf_op jit(solution)/shard_map/all_to_all | solution.py:50
  (121 shorter events, 92.5 us)
Async XLA Ops:
  7.4 35.8 %all-gather.16.cloned.1.call-start = ((), (), s32[]{:S(2)}) async-start(), calls=%async_computation.15 | async-start | bytes 1310720 | tf_op jit(solution)/shard_map/all_gather | solution.py:22
  8.3 34.9 %copy-start.6 = (f32[3,11,1024]{2,0,1:T(4,128)}, f32[3,11,1024]{2,0,1:T(4,128)S(1)}, u32[]{:S(2)}) copy-start(f32[3,11,1024]{2,0,1:T(4,128)S(1)} %reshape.514) | copy-start | bytes 405508
  16.4 65.3 %all-gather.20.cloned.1.call-start = ((), (), s32[]{:S(2)}) async-start(), calls=%async_computation.17 | async-start | bytes 1474560 | tf_op jit(solution)/shard_map/all_gather | solution.py:22
  23.1 62.0 %all-gather.18.cloned.1.call-start = ((), (), s32[]{:S(2)}) async-start(), calls=%async_computation.16 | async-start | bytes 3145728 | tf_op jit(solution)/shard_map/all_gather | solution.py:22
  43.2 131.5 %reduce-scatter.4.cloned.1.call-start = ((), (), s32[]{:S(2)}) async-start(), calls=%async_computation.12 | async-start | bytes 4456448 | tf_op jit(solution)/shard_map/reduce_scatter | solution.py:79
  77.9 31.5 %all-to-all-start.4 = ((bf16[8,9,64,128]{3,2,1,0:T(8,128)(2,1)}), bf16[8,9,64,128]{3,2,1,0:T(8,128)(2,1)S(1)}, u32[]{:S(2)}, u32[]{:S(2)}) async-start(bf16[8,9,64,128]{3,2,1,0:T(8,128)(2,1)} %broadcast_in_dim.15), calls=%async_computation.5 | async-start | bytes 2359296 | tf_op jit(solution)/shard_map/all_to_all | solution.py:35
  81.6 131.0 %all-gather.22.cloned.1.call-start = ((), (), s32[]{:S(2)}) async-start(), calls=%async_computation.18 | async-start | bytes 3538944 | tf_op jit(solution)/shard_map/all_gather | solution.py:22
  109.5 62.5 %all-to-all-start = ((f32[8,8,64,128]{3,2,1,0:T(8,128)}), f32[8,8,64,128]{3,2,1,0:T(8,128)}, u32[]{:S(2)}, u32[]{:S(2)}) async-start(f32[8,8,64,128]{3,2,1,0:T(8,128)} %fusion.25), calls=%async_computation | async-start | bytes 4194304 | tf_op jit(solution)/shard_map/all_to_all | solution.py:50
  114.0 133.0 %all-gather.24.cloned.1.call-start = ((), (), s32[]{:S(2)}) async-start(), calls=%async_computation.19 | async-start | bytes 1638400 | tf_op jit(solution)/shard_map/all_gather | solution.py:22
  174.6 10.7 %copy-start.5 = (f32[64,8,128]{2,0,1:T(8,128)S(1)}, f32[64,8,128]{2,0,1:T(8,128)}, u32[]{:S(2)}) copy-start(f32[64,8,128]{2,0,1:T(8,128)} %reduce-scatter.4.cloned.1.call-done) | copy-start | bytes 786436
  178.3 15.5 %all-to-all-start.2 = ((f32[8,64,128]{2,1,0:T(8,128)}), f32[8,64,128]{2,1,0:T(8,128)S(1)}, u32[]{:S(2)}, u32[]{:S(2)}) async-start(f32[8,64,128]{2,1,0:T(8,128)} %convolution_bitcast_fusion.3), calls=%async_computation.3 | async-start | bytes 524288 | tf_op jit(solution)/shard_map/all_to_all | solution.py:50
  185.1 116.0 %reduce-scatter.6.cloned.1.call-start = ((), (), s32[]{:S(2)}) async-start(), calls=%async_computation.13 | async-start | bytes 5013504 | tf_op jit(solution)/shard_map/reduce_scatter | solution.py:79
  208.3 33.6 %all-to-all-start.7 = ((bf16[8,10,64,128]{3,2,1,0:T(8,128)(2,1)}), bf16[8,10,64,128]{3,2,1,0:T(8,128)(2,1)}, u32[]{:S(2)}, u32[]{:S(2)}) async-start(bf16[8,10,64,128]{3,2,1,0:T(8,128)(2,1)} %broadcast_in_dim.16), calls=%async_computation.9 | async-start | bytes 2621440 | tf_op jit(solution)/shard_map/all_to_all | solution.py:35
  241.9 56.5 %all-to-all-start.3 = ((f32[8,9,64,128]{3,2,1,0:T(8,128)}), f32[8,9,64,128]{3,2,1,0:T(8,128)}, u32[]{:S(2)}, u32[]{:S(2)}) async-start(f32[8,9,64,128]{3,2,1,0:T(8,128)} %copy.60), calls=%async_computation.4 | async-start | bytes 4718592 | tf_op jit(solution)/shard_map/all_to_all | solution.py:50
  246.9 82.1 %all-gather.26.cloned.1.call-start = ((), (), s32[]{:S(2)}) async-start(), calls=%async_computation.20 | async-start | bytes 3932160 | tf_op jit(solution)/shard_map/all_gather | solution.py:22
  300.2 17.7 %copy-start.7 = (f32[3,64,128]{2,1,0:T(8,128)S(1)}, f32[3,64,128]{2,1,0:T(8,128)}, u32[]{:S(2)}) copy-start(f32[3,64,128]{2,1,0:T(8,128)} %param.28) | copy-start | bytes 294916
  301.1 8.3 %copy-start.4 = (f32[64,9,128]{2,0,1:T(8,128)S(1)}, f32[64,9,128]{2,0,1:T(8,128)}, u32[]{:S(2)}) copy-start(f32[64,9,128]{2,0,1:T(8,128)} %reduce-scatter.6.cloned.1.call-done) | copy-start | bytes 884740
  305.1 12.8 %all-to-all-start.5 = ((f32[8,64,128]{2,1,0:T(8,128)}), f32[8,64,128]{2,1,0:T(8,128)S(1)}, u32[]{:S(2)}, u32[]{:S(2)}) async-start(f32[8,64,128]{2,1,0:T(8,128)} %convolution_bitcast_fusion.2), calls=%async_computation.7 | async-start | bytes 524288 | tf_op jit(solution)/shard_map/all_to_all | solution.py:50
  309.1 115.0 %reduce-scatter.8.cloned.1.call-start = ((), (), s32[]{:S(2)}) async-start(), calls=%async_computation.14 | async-start | bytes 5570560 | tf_op jit(solution)/shard_map/reduce_scatter | solution.py:79
  329.1 2.9 copy-start.1
  339.2 6.7 %copy-start.8 = (s32[4]{0:T(128)S(1)}, s32[4]{0:T(128)}, u32[]{:S(2)}) copy-start(s32[4]{0:T(128)} %constant.327.clone.1) | copy-start | bytes 52
  339.2 65.0 %all-to-all-start.6 = ((f32[8,10,64,128]{3,2,1,0:T(8,128)}), f32[8,10,64,128]{3,2,1,0:T(8,128)}, u32[]{:S(2)}, u32[]{:S(2)}) async-start(f32[8,10,64,128]{3,2,1,0:T(8,128)} %copy.65), calls=%async_computation.8 | async-start | bytes 5242880 | tf_op jit(solution)/shard_map/all_to_all | solution.py:50
  424.2 10.5 %copy-start.3 = (f32[64,10,128]{2,0,1:T(8,128)S(1)}, f32[64,10,128]{2,0,1:T(8,128)}, u32[]{:S(2)}) copy-start(f32[64,10,128]{2,0,1:T(8,128)} %reduce-scatter.8.cloned.1.call-done) | copy-start | bytes 983044
  428.4 15.0 %all-to-all-start.8 = ((f32[8,64,128]{2,1,0:T(8,128)}), f32[8,64,128]{2,1,0:T(8,128)S(1)}, u32[]{:S(2)}, u32[]{:S(2)}) async-start(f32[8,64,128]{2,1,0:T(8,128)} %convolution_bitcast_fusion.1), calls=%async_computation.11 | async-start | bytes 524288 | tf_op jit(solution)/shard_map/all_to_all | solution.py:50
  (2 other events, 4.8 us)
Sparse Core Ops, SparseCore 0:
  16.5 26.6 all-gather.15
  44.8 24.6 all-gather.19
  71.2 13.8 all-gather.17
  86.6 15.0 all-gather.21
  161.9 25.7 all-gather.23
  249.1 17.0 all-gather.25
Sparse Core Ops, SparseCore 1:
  74.9 82.8 reduce-scatter.3
  205.1 91.0 reduce-scatter.5
  329.1 95.0 reduce-scatter.7
where the time goes:
time: 454 us; the launch traced here: 452 us
  waiting for transfers between devices  198 us (44%)
  blocking collectives  79.6 us (18%)
  matrix products  54.8 us (12%)
  starting transfers between devices  39.8 us (9%)
  local copies, waits for them, and re-layouts  38.5 us (8%)
  other arithmetic  25.3 us (6%)
  between operations  15.4 us (3%)
    all_to_all x6, waiting for transfers between devices, summed_on_arrival(): lax.all_to_all(tiles, axis, split_axis=0, concat_axis=0, tiled=True)  121 us
    all_gather x3, blocking collectives, stacked_from(): tiles = lax.all_gather(tiles, axes[k])  57.9 us
    all_to_all x2, waiting for transfers between devices, from_everyone(): return lax.all_to_all(copies, axis, split_axis=0, concat_axis=0, tiled=True)  36.1 us
    all_to_all x6, starting transfers between devices, summed_on_arrival(): lax.all_to_all(tiles, axis, split_axis=0, concat_axis=0, tiled=True)  31.2 us
    dot_general x3, matrix products, per_device(): jnp.einsum('akw,akbj->wbj', upper_full, known, precision=lax.Precision.HI...  26.6 us
    all_gather x6, waiting for transfers between devices, stacked_from(): tiles = lax.all_gather(tiles, axes[k])  23 us
    all_to_all x1, blocking collectives, from_everyone(): return lax.all_to_all(copies, axis, split_axis=0, concat_axis=0, tiled=True)  21.7 us
    reduce_scatter x3, waiting for transfers between devices, per_device(): row_sum = lax.psum_scatter(row_terms, COL, scatter_dimension=0, tiled=True)  17.1 us
  transfers between devices with their start and end apart: 17, of which 10 were waited for; matrix products, arithmetic and copies ran while one was open for 24% of the time, Pallas kernels for 0%

commit v1 on v0

v1 whole, which is shorter than its diff:
```python
import jax
import jax.numpy as jnp
from jax import lax
from jax.experimental import pallas as pl
from jax.experimental.pallas import tpu as pltpu
from jax.sharding import Mesh
from jax.sharding import PartitionSpec as P

F32 = jnp.float32
BF16 = jnp.bfloat16
BLK = 128
NSUP = 3
NSEG = 11
ROW = ("yh", "z")
COL = ("x", "yl", "core")
ORDER = (3, 4, 5, 6, 7, 8, 9, 10, 2, 1)
NK = {2: 8, 1: 9, 0: 10}
KC = {2: 1024, 1: 1152, 0: 1280}
KR = {2: 512, 1: 576, 0: 640}
UL = {2: 512, 1: 640, 0: 640}
BUF = {2: 0, 1: 1, 0: 0}
MESH = pl.DeviceIdType.MESH


def nt(a, b):
    return lax.dot_general(a, b, (((1,), (1,)), ((), ())), preferred_element_type=F32)


def nn(a, b):
    return lax.dot_general(a, b, (((1,), (0,)), ((), ())), preferred_element_type=F32)


def split(v):
    hi = v.astype(BF16)
    return hi, (v - hi.astype(F32)).astype(BF16)


class Sems:
    def __init__(self, ref):
        self.ref, self.used = ref, 0

    def take(self):
        self.used += 1
        return self.ref.at[self.used - 1]


def kernel(mr, mc, reg, lin, uin, diag, out, a32, kh, kl, ls2, ls1, ls0, us2, us1, us0, cp, rp, rcl,
           rrl, rxl, ryl, crl, cxl, cyl, dp, dl, cf, rf, df, rh, rl, send_sem, recv_sem, out_sem):
    ls = {2: ls2, 1: ls1, 0: ls0}
    us = {2: us2, 1: us1, 0: us0}
    yh, z = lax.axis_index("yh"), lax.axis_index("z")
    x, yl, core = lax.axis_index("x"), lax.axis_index("yl"), lax.axis_index("core")
    sends, recvs, outs = Sems(send_sem), Sems(recv_sem), Sems(out_sem)
    out_copies = []

    def remote(src, dst, where):
        return pltpu.make_async_remote_copy(
            src_ref=src, dst_ref=dst, send_sem=sends.take(), recv_sem=recvs.take(),
            device_id=where, device_id_type=MESH)

    def to_out(src, dst):
        copy = pltpu.make_async_copy(src, dst, outs.take())
        copy.start()
        out_copies.append(copy)

    def ring_places(axis, here):
        return {axis: lax.rem(here + 1, 4)}, {axis: lax.rem(here + 3, 4)}

    loads = [pltpu.make_async_copy(reg.at[:, :, b, :], a32.at[b], outs.take()) for b in range(8)]
    for copy in loads:
        copy.start()
    barrier = pltpu.get_barrier_semaphore()
    peers = [{"yl": 1 - yl}, {"core": 1 - core}, *ring_places("x", x)]
    others = [(a, d) for a in range(2) for d in range(4) if (a, d) != (0, 0)]
    peers += [{"yh": lax.rem(yh + a, 2), "z": lax.rem(z + d, 4)} for a, d in others]
    for peer in peers:
        pl.semaphore_signal(barrier, inc=1, device_id=peer, device_id_type=MESH)
    pl.semaphore_wait(barrier, len(peers))

    def gather(src, slab, axis, here, pair_axis, pair, to_core):
        up, down = ring_places(axis, here)
        hp, hm, h2 = lax.rem(here + 1, 4), lax.rem(here + 3, 4), lax.rem(here + 2, 4)
        other = {pair_axis: 1 - pair}
        oq = 1 - pair
        started, crossed = [], []

        def go(copy):
            copy.start()
            started.append(copy)
            return copy

        def cross(h, q):
            if to_core:
                crossed.append(go(remote(slab(h, q), slab(h, q), {"core": 1 - core})))

        slab(here, pair)[...] = src[...]
        m_pair = go(remote(src, slab(here, pair), other))
        m_op = go(remote(src, slab(here, pair), up))
        m_om = go(remote(src, slab(here, pair), down))
        if to_core:
            crossed.append(go(remote(src, slab(here, pair), {"core": 1 - core})))
        yield
        m_pair.wait_recv()
        m_tp = go(remote(slab(here, oq), slab(here, oq), up))
        m_tm = go(remote(slab(here, oq), slab(here, oq), down))
        cross(here, oq)
        m_op.wait_recv()
        m_rp = go(remote(slab(hm, pair), slab(hm, pair), up))
        cross(hm, pair)
        m_om.wait_recv()
        cross(hp, pair)
        yield
        m_tm.wait_recv()
        m_rm = go(remote(slab(hp, oq), slab(hp, oq), down))
        cross(hp, oq)
        m_tp.wait_recv()
        cross(hm, oq)
        yield
        m_rp.wait_recv()
        cross(h2, pair)
        m_rm.wait_recv()
        cross(h2, oq)
        yield
        for copy in crossed:
            copy.wait_recv()
        for copy in started:
            copy.wait_send()
        yield

    def gather_l(s):
        slab = ls[s]
        return gather(lin.at[s, :, 0:KC[s]], lambda h, q: slab.at[(h * 2 + q) * 2 + core], "x", x, "yl", yl, True)

    def gather_u(s):
        slab = us[s]
        return gather(uin.at[s, :, 0:UL[s]], lambda h, q: slab.at[q * 4 + h], "z", z, "yh", yh, False)

    def reduce_ring(blk, relay, side, last, axis, here, pair_axis, pair, pre, finish):
        up, down = ring_places(axis, here)
        hp, hm, h2 = lax.rem(here + 1, 4), lax.rem(here + 3, 4), lax.rem(here + 2, 4)
        started = []

        def go(src, dst, where):
            copy = remote(src, dst, where)
            copy.start()
            started.append(copy)
            return copy

        pre(h2, 0)
        m_rp = go(blk(h2, 0), relay(0), up)
        pre(h2, 1)
        m_rm = go(blk(h2, 1), relay(1), down)
        pre(hp, 1)
        m_ep = go(blk(hp, 1), side(0, 1), up)
        pre(hm, 0)
        m_em = go(blk(hm, 0), side(1, 0), down)
        pre(hp, 0)
        pre(hm, 1)
        pre(here, 0)
        pre(here, 1)
        yield
        m_rp.wait_recv()
        blk(hp, 0)[...] += relay(0)[...]
        m_fp = go(blk(hp, 0), side(0, 0), up)
        m_rm.wait_recv()
        blk(hm, 1)[...] += relay(1)[...]
        m_fm = go(blk(hm, 1), side(1, 1), down)
        yield
        for copy in (m_ep, m_em, m_fp, m_fm):
            copy.wait_recv()
        oq = 1 - pair
        blk(here, oq)[...] += side(0, oq)[...] + side(1, oq)[...]
        m_y = go(blk(here, oq), last, {pair_axis: oq})
        blk(here, pair)[...] += side(0, pair)[...] + side(1, pair)[...]
        yield
        m_y.wait_recv()
        finish()
        for copy in started:
            copy.wait_send()
        yield

    def reduce_rows(s):
        b, n = BUF[s], KC[s]
        blk = lambda h, q: rp.at[b, core, h * 2 + q, :, 0:n]
        over = remote(rp.at[b, 1 - core, :, :, 0:n], rcl.at[b, :, :, 0:n], {"core": 1 - core})
        over.start()
        yield
        over.wait_recv()

        def pre(h, q):
            blk(h, q)[...] += rcl[b, h * 2 + q, :, 0:n]

        def finish():
            for i in range(NK[s]):
                at = slice(i * 128, (i + 1) * 128)
                v = mc[s, i] * (rp[b, core, x * 2 + yl, :, at] + ryl[b, :, at])
                rf[s, :, at] = v
                hi, lo = split(v)
                rh[:, at] = hi
                rl[:, at] = lo
                if s > 0:
                    r0 = 512 + 64 * (2 - s)
                    kh[r0 : r0 + 64, at] = hi
                    kl[r0 : r0 + 64, at] = lo
                to_out(rf.at[s, :, at], out.at[s, :, ORDER[i], :])

        yield from reduce_ring(
            blk, lambda d: rrl.at[b, d, :, 0:n], lambda d, q: rxl.at[b, d, q, :, 0:n], ryl.at[b, :, 0:n],
            "x", x, "yl", yl, pre, finish)
        over.wait_send()
        yield

    def reduce_cols(s):
        b, n = BUF[s], KR[s]
        blk = lambda h, q: cp.at[b, q * 4 + h, 0:n, :]

        def finish():
            for i in range(NK[s]):
                at = slice(i * 64, (i + 1) * 64)
                v = mr[s, i] * (cp[b, yh * 4 + z, at, :] + cyl[b, at, :])
                cf[s, i] = v
                if s > 0:
                    c0 = 1024 + 128 * (2 - s)
                    hi, lo = split(v)
                    kh[at, c0 : c0 + 128] = hi
                    kl[at, c0 : c0 + 128] = lo
            to_out(cf.at[s, 0:8], out.at[3:11, :, s, :])
            for i in range(8, NK[s]):
                to_out(cf.at[s, i], out.at[ORDER[i], :, s, :])

        yield from reduce_ring(
            blk, lambda d: crl.at[b, d, 0:n, :], lambda d, q: cxl.at[b, d, q, 0:n, :], cyl.at[b, 0:n, :],
            "z", z, "yh", yh, lambda h, q: None, finish)

    def reduce_diag(s):
        b, n = BUF[s], KC[s]

        @pl.loop(0, 4)
        def _(t):
            w = ls[s][pl.ds(4 * t, 4), :, :].reshape(256, n)
            acc = nt(rh[:, 0:n], w) + nt(rl[:, 0:n], w)
            dp[b, 2 * t] = acc[:, 0:128]
            dp[b, 2 * t + 1] = acc[:, 128:256]

        started = []
        for k, (a, d) in enumerate(others):
            py, pz = lax.rem(yh + a, 2), lax.rem(z + d, 4)
            copy = remote(dp.at[b, py * 4 + pz], dl.at[b, k], {"yh": py, "z": pz})
            copy.start()
            started.append(copy)
        yield
        for copy in started:
            copy.wait_recv()
        v = diag[s] - dp[b, yh * 4 + z]
        for k in range(7):
            v = v - dl[b, k]
        df[s] = v
        if s > 0:
            r0, c0 = 512 + 64 * (2 - s), 1024 + 128 * (2 - s)
            hi, lo = split(v)
            kh[r0 : r0 + 64, c0 : c0 + 128] = hi
            kl[r0 : r0 + 64, c0 : c0 + 128] = lo
        to_out(df.at[s], out.at[s, :, s, :])
        for copy in started:
            copy.wait_send()
        yield

    def store_r(b, t, acc, at):
        for q in range(4):
            rp[b, q % 2, 2 * t + q // 2, :, at] = acc[64 * q : 64 * (q + 1), :]

    def heavy_c(s):
        b = BUF[s]

        @pl.loop(0, 4)
        def _(t):
            w = ls[s][pl.ds(4 * t, 4), :, 0:1024].reshape(256, 1024)
            acc = nt(kh[0:512, 0:1024], w) + nt(kl[0:512, 0:1024], w)
            cp[b, 2 * t, 0:512, :] = acc[:, 0:128]
            cp[b, 2 * t + 1, 0:512, :] = acc[:, 128:256]

    def heavy_r(s):
        b = BUF[s]

        @pl.loop(0, 4)
        def _(t):
            w = us[s][pl.ds(2 * t, 2), :, 0:512].reshape(256, 512)
            acc = nn(w, kh[0:512, 0:1024]) + nn(w, kl[0:512, 0:1024])
            store_r(b, t, acc, slice(0, 1024))

    def extra(s):
        b, n, m = BUF[s], KC[s], KR[s]

        @pl.loop(0, 4)
        def _(t):
            w = us[s][pl.ds(2 * t, 2), :, :].reshape(256, 640)
            acc = nn(w[:, 512:640], kh[512:640, 0:1024]) + nn(w[:, 512:640], kl[512:640, 0:1024])
            for q in range(4):
                rp[b, q % 2, 2 * t + q // 2, :, 0:1024] += acc[64 * q : 64 * (q + 1), :]
            acc = nn(w, kh[0:640, 1024:n]) + nn(w, kl[0:640, 1024:n])
            store_r(b, t, acc, slice(1024, n))

        @pl.loop(0, 4)
        def _(t):
            w = ls[s][pl.ds(4 * t, 4), :, :].reshape(256, n)
            acc = nt(kh[0:512, 1024:n], w[:, 1024:n]) + nt(kl[0:512, 1024:n], w[:, 1024:n])
            cp[b, 2 * t, 0:512, :] += acc[:, 0:128]
            cp[b, 2 * t + 1, 0:512, :] += acc[:, 128:256]
            acc = nt(kh[512:m, 0:n], w) + nt(kl[512:m, 0:n], w)
            cp[b, 2 * t, 512:m, :] = acc[:, 0:128]
            cp[b, 2 * t + 1, 512:m, :] = acc[:, 128:256]

    gl = {s: gather_l(s) for s in (2, 1, 0)}
    gu = {s: gather_u(s) for s in (2, 1, 0)}

    def step_gather(s):
        next(gl[s])
        next(gu[s])

    step_gather(2)
    for b in range(8):
        loads[b].wait()
        to_out(a32.at[b], out.at[3:11, :, 3 + b, :])
        hi, lo = split(a32[b].reshape(512, 128))
        kh[0:512, b * 128 : (b + 1) * 128] = hi
        kl[0:512, b * 128 : (b + 1) * 128] = lo
    for ref in (kh, kl):
        ref[512:640, :] = jnp.zeros((128, 1280), BF16)
        ref[0:512, 1024:1280] = jnp.zeros((512, 256), BF16)
    for _ in range(4):
        step_gather(2)
    step_gather(1)
    heavy_r(2)
    heavy_c(2)
    for s in (2, 1, 0):
        t = s - 1
        if t >= 0:
            after = [lambda: step_gather(t)] * 4 + [lambda: heavy_r(t), lambda: heavy_c(t)]
            if t == 1:
                after.append(lambda: step_gather(0))
        else:
            after = []

        def fill(count):
            for _ in range(count):
                if after:
                    after.pop(0)()

        r, c = reduce_rows(s), reduce_cols(s)
        next(r)
        next(c)
        fill(1)
        next(r)
        next(c)
        fill(1)
        next(r)
        next(c)
        fill(2)
        next(r)
        next(c)
        fill(1)
        next(r)
        d = reduce_diag(s)
        next(d)
        next(r)
        fill(9)
        next(d)
        if t >= 0:
            extra(t)
    for copy in out_copies:
        copy.wait()


def per_device(region, l_panels, u_panels, diag_inv, pattern):
    row_index = lax.axis_index(ROW)
    col_index = lax.axis_index(COL)
    order = jnp.array(ORDER)
    picked = pattern[:, order, :]
    rows_block = col_index // 2
    mr = lax.dynamic_slice_in_dim(picked, rows_block, 1, 2)[:, :, 0]
    mc = lax.dynamic_slice_in_dim(picked, row_index, 1, 2)[:, :, 0]

    def in_order(value, dim):
        cut = lambda a, b: lax.slice_in_dim(value, a, b, axis=dim)
        return jnp.concatenate([cut(3, 11), cut(2, 3), cut(1, 2)], axis=dim)

    lin = in_order(l_panels, 2) * mc.astype(BF16)[:, None, :, None]
    lin = lin.reshape(3, 64, 1280)
    uin = in_order(u_panels, 1) * mr.astype(BF16)[:, :, None, None]
    uin = uin.transpose(0, 3, 1, 2).reshape(3, 128, 640)
    smem = pl.BlockSpec(memory_space=pltpu.SMEM)
    vmem = pl.BlockSpec(memory_space=pltpu.VMEM)
    hbm = pl.BlockSpec(memory_space=pl.ANY)
    sem = lambda n: pltpu.SemaphoreType.DMA((n,))
    return pl.pallas_call(
        kernel,
        name="selinv",
        out_shape=jax.ShapeDtypeStruct((NSEG, 64, NSEG, 128), F32),
        in_specs=[smem, smem, hbm, vmem, vmem, vmem],
        out_specs=hbm,
        scratch_shapes=[
            pltpu.VMEM((8, 8, 64, 128), F32),
            pltpu.VMEM((640, 1280), BF16),
            pltpu.VMEM((640, 1280), BF16),
            pltpu.VMEM((16, 64, KC[2]), BF16),
            pltpu.VMEM((16, 64, KC[1]), BF16),
            pltpu.VMEM((16, 64, KC[0]), BF16),
            pltpu.VMEM((8, 128, UL[2]), BF16),
            pltpu.VMEM((8, 128, UL[1]), BF16),
            pltpu.VMEM((8, 128, UL[0]), BF16),
            pltpu.VMEM((2, 8, 640, 128), F32),
            pltpu.VMEM((2, 2, 8, 64, 1280), F32),
            pltpu.VMEM((2, 8, 64, 1280), F32),
            pltpu.VMEM((2, 2, 64, 1280), F32),
            pltpu.VMEM((2, 2, 2, 64, 1280), F32),
            pltpu.VMEM((2, 64, 1280), F32),
            pltpu.VMEM((2, 2, 640, 128), F32),
            pltpu.VMEM((2, 2, 2, 640, 128), F32),
            pltpu.VMEM((2, 640, 128), F32),
            pltpu.VMEM((2, 8, 64, 128), F32),
            pltpu.VMEM((2, 7, 64, 128), F32),
            pltpu.VMEM((3, 10, 64, 128), F32),
            pltpu.VMEM((3, 64, 1280), F32),
            pltpu.VMEM((3, 64, 128), F32),
            pltpu.VMEM((64, 1280), BF16),
            pltpu.VMEM((64, 1280), BF16),
            sem(160),
            sem(160),
            sem(64),
        ],
        compiler_params=pltpu.CompilerParams(
            collective_id=0, has_side_effects=True, vmem_limit_bytes=64000 * 1024),
    )(-mr.astype(F32), -mc.astype(F32), region, lin, uin, diag_inv)


def solution(mesh):
    split_mesh = Mesh(mesh.devices.reshape(2, 4, 4, 2, 2), ROW + COL)
    in_specs = (
        P(None, COL, None, ROW),
        P(None, COL, None, ROW),
        P(None, None, COL, ROW),
        P(None, COL, ROW),
        P(),
    )
    out_specs = P(None, COL, None, ROW)
    return jax.shard_map(
        per_device, mesh=split_mesh, in_specs=in_specs, out_specs=out_specs, check_vma=False
    )
```

time: 454 us -> 195 us (0.43)
  waiting for transfers between devices: 198 us -> 0 us
  Pallas kernels: 0 us -> 177 us
  blocking collectives: 79.6 us -> 0 us
  matrix products: 54.8 us -> 0 us
  starting transfers between devices: 39.8 us -> 0 us
  local copies, waits for them, and re-layouts: 38.5 us -> 13.5 us
  other arithmetic: 25.3 us -> 1.81 us
  between operations: 15.4 us -> 0.05 us
    pallas_call x0 -> x1, Pallas kernels: none -> 177 us  [per_device(): pl.pallas_call(kernel, name='selinv', out_shape=jax.ShapeDtypeStruct((NSE...]
    all_to_all x8 -> x0, waiting for transfers between devices: 157 us -> none  [the longest x6 121 us: summed_on_arrival(): lax.all_to_all(tiles, axis, split_axis=0, concat_axis=0, tiled=True)]
    all_gather x3 -> x0, blocking collectives: 57.9 us -> none  [stacked_from(): tiles = lax.all_gather(tiles, axes[k])]
    dot_general x9 -> x0, matrix products: 54.8 us -> none  [the longest x3 26.6 us: per_device(): jnp.einsum('akw,akbj->wbj', upper_full, known, precision=lax.Precision.HI...]
    all_to_all x8 -> x0, starting transfers between devices: 39.1 us -> none  [the longest x6 31.2 us: summed_on_arrival(): lax.all_to_all(tiles, axis, split_axis=0, concat_axis=0, tiled=True)]
    all_gather x6 -> x0, waiting for transfers between devices: 23 us -> none  [stacked_from(): tiles = lax.all_gather(tiles, axes[k])]
    all_to_all x1 -> x0, blocking collectives: 21.7 us -> none  [from_everyone(): return lax.all_to_all(copies, axis, split_axis=0, concat_axis=0, tiled=True)]
    reduce_scatter x3 -> x0, waiting for transfers between devices: 17.1 us -> none  [per_device(): row_sum = lax.psum_scatter(row_terms, COL, scatter_dimension=0, tiled=True)]
  transfers between devices with their start and end apart: 17 -> 0, of which waited for: 10 -> 0; matrix products, arithmetic and copies ran while one was open for 24% -> 0% of each run, Pallas kernels for 0% -> 0%
where the time goes in v1:
time: 195 us; the launch traced here: 193 us
  Pallas kernels  177 us (91%)
  local copies, waits for them, and re-layouts  13.5 us (7%)
    pallas_call x1, Pallas kernels, per_device(): pl.pallas_call(kernel, name='selinv', out_shape=jax.ShapeDtypeStruct((NSE...  177 us
    pallas_call x1, local copies, waits for them, and re-layouts, per_device(): pl.pallas_call(kernel, name='selinv', out_shape=jax.ShapeDtypeStruct((NSE...  5.76 us

profile of v1, /device:TPU:0, one launch (start us, length us, event | category | flops | bytes accessed | tf_op | source)
XLA Modules:
  0.0 192.8 jit_solution(16755846316842854408)
XLA Ops:
  0.0 0.7 pad_clamp_fusion
  0.7 0.8 copy.10
  1.5 0.6 gather_fusion
  2.0 0.1 fusion
  2.1 0.1 copy.15
  2.3 0.1 copy.14
  2.4 0.1 broadcast_bitcast_fusion
  2.5 0.1 negate_bitcast_fusion
  2.6 0.7 copy.12
  3.3 0.7 copy.11
  3.9 0.8 fusion.3
  4.8 0.8 fusion.2
  5.6 1.0 slice.18
  6.6 0.9 bitcast_multiply_fusion.lin
  7.5 1.0 slice.21
  8.5 0.1 maximum_multiply_fusion
  8.6 1.0 copy.16.uin
  9.6 177.4 %selinv.1 = f32[11,64,11,128]{3,2,1,0:T(8,128)} custom-call(f32[3,10]{1,0:T(4,128)} %bitcast.28, f32[3,10]{1,0:T(4,128)} %bitcast.27, f32[8,64,8,128]{3,2,1,0:T(8,128)} %reg.1, bf16[3,64,1280]{2,1,0:T(8,128)(2,1)} %bitcast_multiply_fusion.lin, bf16[3,128,640]{2,1,0:T(8,128)(2,1)} %copy.16.uin, f32[3,64,128]{2,1,0:T(8,128)} %diag.1), custom_call_target="tpu_custom_call" | custom-call | tf_op jit(solution)/shard_map/selinv/pallas_call | solution.py:395
  187.1 5.8 %copy.17 = f32[11,64,11,128]{3,1,2,0:T(8,128)} copy(f32[11,64,11,128]{3,2,1,0:T(8,128)} %selinv.1) | data formatting | bytes 7929856 | tf_op jit(solution)/shard_map/selinv/pallas_call | solution.py:395
  (1 shorter events, 0.0 us)

commit v2 on v1

v2 whole, which is shorter than its diff:
```python
import jax
import jax.numpy as jnp
from jax import lax
from jax.experimental import pallas as pl
from jax.experimental.pallas import tpu as pltpu
from jax.sharding import Mesh
from jax.sharding import PartitionSpec as P

F32 = jnp.float32
BF16 = jnp.bfloat16
I16 = jnp.int16
NSEG = 11
ROW = ("yh", "z")
COL = ("x", "yl", "core")
KC = {2: 1024, 1: 1152, 0: 1280}
KR = {2: 512, 1: 576, 0: 640}
U0 = {2: 128, 1: 0, 0: 0}
BUF = {2: 0, 1: 1, 0: 0}
TOP = 32700.0
MESH = pl.DeviceIdType.MESH


def nt(a, b):
    return lax.dot_general(a, b, (((1,), (1,)), ((), ())), preferred_element_type=F32)


def nn(a, b):
    return lax.dot_general(a, b, (((1,), (0,)), ((), ())), preferred_element_type=F32)


def split(v):
    hi = v.astype(BF16)
    return hi, (v - hi.astype(F32)).astype(BF16)


def folded(v):
    return v.reshape(v.shape[0] // 8, 8, 128)


class Sems:
    def __init__(self, ref):
        self.ref, self.used = ref, 0

    def take(self):
        self.used += 1
        return self.ref.at[self.used - 1]


def kernel(pattern, reg, lin, uin, diag, out, a32, kh, kl, ls2, ls1, ls0, us2, us1, us0, cp, rp, rcl,
           rq_out, rq_in, rs_out, rs_in, cq_out, cq_in, cs_out, cs_in, dp, dl, cf, rf, df, rh, rl,
           send_sem, recv_sem, out_sem):
    ls = {2: ls2, 1: ls1, 0: ls0}
    us = {2: us2, 1: us1, 0: us0}
    yh, z = lax.axis_index("yh"), lax.axis_index("z")
    x, yl, core = lax.axis_index("x"), lax.axis_index("yl"), lax.axis_index("core")
    sends, recvs, outs = Sems(send_sem), Sems(recv_sem), Sems(out_sem)
    out_copies = []

    def mask_row(s, i):
        return pattern[s, i + 1, x * 2 + yl].astype(F32)

    def mask_col(s, i):
        return pattern[s, i + 1, yh * 4 + z].astype(F32)

    def remote(src, dst, where):
        return pltpu.make_async_remote_copy(
            src_ref=src, dst_ref=dst, send_sem=sends.take(), recv_sem=recvs.take(),
            device_id=where, device_id_type=MESH)

    def to_out(src, dst):
        copy = pltpu.make_async_copy(src, dst, outs.take())
        copy.start()
        out_copies.append(copy)

    def ring_places(axis, here):
        return {axis: lax.rem(here + 1, 4)}, {axis: lax.rem(here + 3, 4)}

    others = [(a, d) for a in range(2) for d in range(4) if (a, d) != (0, 0)]
    with jax.named_scope("signal"):
        barrier = pltpu.get_barrier_semaphore()
        peers = [{"yl": 1 - yl}, {"core": 1 - core}, *ring_places("x", x)]
        peers += [{"yh": lax.rem(yh + a, 2), "z": lax.rem(z + d, 4)} for a, d in others]
        for peer in peers:
            pl.semaphore_signal(barrier, inc=1, device_id=peer, device_id_type=MESH)
    loads = [pltpu.make_async_copy(reg.at[:, :, b, :], a32.at[b], outs.take()) for b in range(8)]
    for copy in loads:
        copy.start()
    with jax.named_scope("own"):
        lane = lax.broadcasted_iota(jnp.int32, (128, 128), 1)
        for s in (2, 1, 0):
            for i in range(s, 10):
                v = lin[s, :, 128 * i : 128 * (i + 1)].astype(F32) * mask_col(s, i)
                ls[s][(x * 2 + yl) * 2 + core, :, 128 * (i - s) : 128 * (i - s + 1)] = v.astype(BF16)
            for i in range(U0[s] // 128, 5):
                m = jnp.where(lane < 64, mask_row(s, 2 * i), mask_row(s, 2 * i + 1))
                v = uin[s, :, 128 * i : 128 * (i + 1)].astype(F32) * m
                us[s][yh * 4 + z, :, 128 * i - U0[s] : 128 * (i + 1) - U0[s]] = v.astype(BF16)
    with jax.named_scope("barrier"):
        pl.semaphore_wait(barrier, len(peers))

    def gather(slab, axis, here, pair_axis, pair, to_core):
        up, down = ring_places(axis, here)
        hp, hm, h2 = lax.rem(here + 1, 4), lax.rem(here + 3, 4), lax.rem(here + 2, 4)
        other = {pair_axis: 1 - pair}
        oq = 1 - pair
        started, crossed = [], []

        def go(copy):
            copy.start()
            started.append(copy)
            return copy

        def cross(h, q):
            if to_core:
                crossed.append(go(remote(slab(h, q), slab(h, q), {"core": 1 - core})))

        src = slab(here, pair)
        m_pair = go(remote(src, slab(here, pair), other))
        m_op = go(remote(src, slab(here, pair), up))
        m_om = go(remote(src, slab(here, pair), down))
        if to_core:
            crossed.append(go(remote(src, slab(here, pair), {"core": 1 - core})))
        yield
        m_pair.wait_recv()
        m_tp = go(remote(slab(here, oq), slab(here, oq), up))
        m_tm = go(remote(slab(here, oq), slab(here, oq), down))
        cross(here, oq)
        m_op.wait_recv()
        m_rp = go(remote(slab(hm, pair), slab(hm, pair), up))
        cross(hm, pair)
        m_om.wait_recv()
        cross(hp, pair)
        yield
        m_tm.wait_recv()
        m_rm = go(remote(slab(hp, oq), slab(hp, oq), down))
        cross(hp, oq)
        m_tp.wait_recv()
        cross(hm, oq)
        yield
        m_rp.wait_recv()
        cross(h2, pair)
        m_rm.wait_recv()
        cross(h2, oq)
        yield
        for copy in crossed:
            copy.wait_recv()
        for copy in started:
            copy.wait_send()
        yield

    def gather_l(s):
        slab = ls[s]
        return gather(lambda h, q: slab.at[(h * 2 + q) * 2 + core], "x", x, "yl", yl, True)

    def gather_u(s):
        slab = us[s]
        return gather(lambda h, q: slab.at[q * 4 + h], "z", z, "yh", yh, False)

    def reduce_ring(tiles, val, q_out, q_in, s_out, s_in, part, axis, here, pair_axis, pair, keep, finish):
        up, down = ring_places(axis, here)
        hp, hm, h2 = lax.rem(here + 1, 4), lax.rem(here + 3, 4), lax.rem(here + 2, 4)
        oq = 1 - pair
        started = []

        def send(k, values, where):
            top = None
            for v in values:
                m = jnp.max(folded(jnp.abs(v)), axis=0)
                top = m if top is None else jnp.maximum(top, m)
            top = jnp.maximum(top, 1e-30)
            s_out[k] = top * (1.0 / TOP)
            inv = TOP / top
            for j, v in enumerate(values):
                q = jnp.round(folded(v) * inv).reshape(v.shape)
                q_out.at[k].at[part(j)][...] = q.astype(jnp.int32).astype(I16)
            pair_of = (remote(q_out.at[k].at[part(None)], q_in.at[k].at[part(None)], where),
                       remote(s_out.at[k], s_in.at[k], where))
            for copy in pair_of:
                copy.start()
            started.extend(pair_of)
            return pair_of

        def arrive(*messages):
            for pair_of in messages:
                for copy in pair_of:
                    copy.wait_recv()

        def got(k, j):
            v = q_in.at[k].at[part(j)][...].astype(F32)
            return (folded(v) * s_in[k]).reshape(v.shape)

        each = range(tiles)
        m_rp = send(0, [val(h2, 0, j) for j in each], up)
        m_rm = send(1, [val(h2, 1, j) for j in each], down)
        m_ep = send(3, [val(hp, 1, j) for j in each], up)
        m_em = send(4, [val(hm, 0, j) for j in each], down)
        yield
        arrive(m_rp)
        m_fp = send(2, [val(hp, 0, j) + got(0, j) for j in each], up)
        arrive(m_rm)
        m_fm = send(5, [val(hm, 1, j) + got(1, j) for j in each], down)
        yield
        arrive(m_ep, m_em, m_fp, m_fm)
        m_y = send(6, [val(here, oq, j) + got(2 + oq, j) + got(4 + oq, j) for j in each], {pair_axis: oq})
        for j in each:
            keep(j, val(here, pair, j) + got(2 + pair, j) + got(4 + pair, j))
        yield
        arrive(m_y)
        for j in each:
            finish(j, got(6, j))
        for copy in started:
            copy.wait_send()
        yield

    def reduce_rows(s):
        b, c0 = BUF[s], 128 * s
        over = remote(rp.at[b, 1 - core, :, :, c0:1280], rcl.at[b, :, :, c0:1280], {"core": 1 - core})
        over.start()
        yield
        over.wait_recv()

        def cols(j):
            return slice(c0 + 128 * j, c0 + 128 * (j + 1))

        def part(j):
            return (slice(0, 64), slice(c0, 1280) if j is None else cols(j))

        def val(h, q, j):
            return rp[b, core, h * 2 + q, :, cols(j)] + rcl[b, h * 2 + q, :, cols(j)]

        def keep(j, v):
            rf[s, :, cols(j)] = v

        def finish(j, last):
            at = cols(j)
            v = -mask_col(s, s + j) * (rf[s, :, at] + last)
            rf[s, :, at] = v
            hi, lo = split(v)
            rh[:, at] = hi
            rl[:, at] = lo
            if s > 0:
                kh[64 * (s - 1) : 64 * s, at] = hi
                kl[64 * (s - 1) : 64 * s, at] = lo
            to_out(rf.at[s, :, at], out.at[s, :, s + j + 1, :])

        yield from reduce_ring(
            10 - s, val, rq_out.at[b], rq_in.at[b], rs_out.at[b], rs_in.at[b], part,
            "x", x, "yl", yl, keep, finish)
        over.wait_send()
        yield

    def reduce_cols(s):
        b, r0 = BUF[s], 64 * s
        rows = slice(r0, 640)

        def keep(j, v):
            cf[s, rows, :] = v

        def finish(j, last):
            for i in range(s, 10):
                at = slice(64 * i, 64 * (i + 1))
                v = -mask_row(s, i) * (cf[s, at, :] + last[64 * (i - s) : 64 * (i - s + 1), :])
                cf[s, at, :] = v
                if s > 0:
                    hi, lo = split(v)
                    kh[at, 128 * (s - 1) : 128 * s] = hi
                    kl[at, 128 * (s - 1) : 128 * s] = lo
                to_out(cf.at[s, at, :], out.at[i + 1, :, s, :])

        yield from reduce_ring(
            1, lambda h, q, j: cp[b, q * 4 + h, rows, :], cq_out.at[b], cq_in.at[b], cs_out.at[b], cs_in.at[b],
            lambda j: (rows, slice(0, 128)), "z", z, "yh", yh, keep, finish)

    def reduce_diag(s):
        b, c0 = BUF[s], 128 * s

        @pl.loop(0, 4)
        def _(t):
            w = ls[s][pl.ds(4 * t, 4), :, :].reshape(256, KC[s])
            acc = nt(rh[:, c0:1280], w) + nt(rl[:, c0:1280], w)
            dp[b, 2 * t] = acc[:, 0:128]
            dp[b, 2 * t + 1] = acc[:, 128:256]

        started = []
        for k, (a, d) in enumerate(others):
            py, pz = lax.rem(yh + a, 2), lax.rem(z + d, 4)
            copy = remote(dp.at[b, py * 4 + pz], dl.at[b, k], {"yh": py, "z": pz})
            copy.start()
            started.append(copy)
        yield
        for copy in started:
            copy.wait_recv()
        v = diag[s] - dp[b, yh * 4 + z]
        for k in range(7):
            v = v - dl[b, k]
        df[s] = v
        if s > 0:
            hi, lo = split(v)
            kh[64 * (s - 1) : 64 * s, 128 * (s - 1) : 128 * s] = hi
            kl[64 * (s - 1) : 64 * s, 128 * (s - 1) : 128 * s] = lo
        to_out(df.at[s], out.at[s, :, s, :])
        for copy in started:
            copy.wait_send()
        yield

    def each_r(s, lo, hi, body):
        @pl.loop(lo, hi)
        def _(t):
            body(us[s][pl.ds(2 * t, 2), :, :].reshape(256, 640 - U0[s]),
                 lambda q: (BUF[s], q % 2, 2 * t + q // 2))

    def each_c(s, lo, hi, body):
        @pl.loop(lo, hi)
        def _(t):
            body(ls[s][pl.ds(4 * t, 4), :, :].reshape(256, KC[s]), BUF[s], 2 * t)

    def heavy_c(s, lo=0, hi=4):
        def body(w, b, r):
            w = w[:, 256 - 128 * s :]
            acc = nt(kh[128:640, 256:1280], w) + nt(kl[128:640, 256:1280], w)
            cp[b, r, 128:640, :] = acc[:, 0:128]
            cp[b, r + 1, 128:640, :] = acc[:, 128:256]

        each_c(s, lo, hi, body)

    def heavy_r(s, lo=0, hi=4):
        def body(w, block):
            w = w[:, 128 - U0[s] :]
            acc = nn(w, kh[128:640, 256:1280]) + nn(w, kl[128:640, 256:1280])
            for q in range(4):
                rp[(*block(q), slice(None), slice(256, 1280))] = acc[64 * q : 64 * (q + 1), :]

        each_r(s, lo, hi, body)

    def extra_r(s):
        def body(w, block):
            w = w[:, 0:128]
            acc = nn(w, kh[0:128, 256:1280]) + nn(w, kl[0:128, 256:1280])
            for q in range(4):
                rp[(*block(q), slice(None), slice(256, 1280))] += acc[64 * q : 64 * (q + 1), :]

        each_r(s, 0, 4, body)

    def extra_c(s):
        def body(w, b, r):
            w = w[:, 0 : 256 - 128 * s]
            at = slice(128 * s, 256)
            acc = nt(kh[128:640, at], w) + nt(kl[128:640, at], w)
            cp[b, r, 128:640, :] += acc[:, 0:128]
            cp[b, r + 1, 128:640, :] += acc[:, 128:256]

        each_c(s, 0, 4, body)

    def tail_r(s):
        def body(w, block):
            at = slice(128 * s, 256)
            acc = nn(w, kh[0:640, at]) + nn(w, kl[0:640, at])
            for q in range(4):
                rp[(*block(q), slice(None), at)] = acc[64 * q : 64 * (q + 1), :]

        each_r(s, 0, 4, body)

    def tail_c(s):
        def body(w, b, r):
            at = slice(64 * s, 128)
            acc = nt(kh[at, 128 * s : 1280], w) + nt(kl[at, 128 * s : 1280], w)
            cp[b, r, at, :] = acc[:, 0:128]
            cp[b, r + 1, at, :] = acc[:, 128:256]

        each_c(s, 0, 4, body)

    gl = {s: gather_l(s) for s in (2, 1, 0)}
    gu = {s: gather_u(s) for s in (2, 1, 0)}

    def step(name, gen):
        with jax.named_scope(name):
            next(gen)

    def step_gather(s):
        step(f"gl{s}", gl[s])
        step(f"gu{s}", gu[s])

    def run(name, f, *args):
        with jax.named_scope(name):
            f(*args)

    step_gather(2)
    with jax.named_scope("split"):
        for b in range(8):
            loads[b].wait()
            to_out(a32.at[b], out.at[3:11, :, 3 + b, :])
            hi, lo = split(a32[b].reshape(512, 128))
            kh[128:640, (b + 2) * 128 : (b + 3) * 128] = hi
            kl[128:640, (b + 2) * 128 : (b + 3) * 128] = lo
        for ref in (kh, kl):
            ref[0:128, :] = jnp.zeros((128, 1280), BF16)
            ref[128:640, 0:256] = jnp.zeros((512, 256), BF16)
    for _ in range(4):
        step_gather(2)
    step_gather(1)
    run("hr2", heavy_r, 2)
    run("hc2", heavy_c, 2)
    for s in (2, 1, 0):
        t = s - 1
        if t >= 0:
            after = [lambda: step_gather(t)] * 4
            after += [lambda: run(f"hr{t}", heavy_r, t), lambda: run(f"hc{t}", heavy_c, t)]
            if t == 1:
                after.append(lambda: step_gather(0))
        else:
            after = []

        def fill(count):
            for _ in range(count):
                if after:
                    after.pop(0)()

        r, c = reduce_rows(s), reduce_cols(s)
        step(f"r{s}", r)
        step(f"c{s}", c)
        fill(1)
        step(f"r{s}", r)
        step(f"c{s}", c)
        fill(1)
        step(f"r{s}", r)
        step(f"c{s}", c)
        fill(2)
        step(f"r{s}", r)
        step(f"c{s}", c)
        fill(1)
        step(f"r{s}", r)
        d = reduce_diag(s)
        step(f"d{s}", d)
        step(f"r{s}", r)
        fill(9)
        if t >= 0:
            run(f"xr{t}", extra_r, t)
            run(f"xc{t}", extra_c, t)
        step(f"d{s}", d)
        if t >= 0:
            run(f"tr{t}", tail_r, t)
            run(f"tc{t}", tail_c, t)
    for copy in out_copies:
        copy.wait()


def per_device(region, l_panels, u_panels, diag_inv, pattern):
    lin = l_panels[:, :, 1:, :].reshape(3, 64, 1280)
    uin = u_panels[:, 1:].transpose(0, 3, 1, 2).reshape(3, 128, 640)
    smem = pl.BlockSpec(memory_space=pltpu.SMEM)
    vmem = pl.BlockSpec(memory_space=pltpu.VMEM)
    hbm = pl.BlockSpec(memory_space=pl.ANY)
    sem = lambda n: pltpu.SemaphoreType.DMA((n,))
    return pl.pallas_call(
        kernel,
        name="selinv",
        out_shape=jax.ShapeDtypeStruct((NSEG, 64, NSEG, 128), F32),
        in_specs=[smem, hbm, vmem, vmem, vmem],
        out_specs=hbm,
        scratch_shapes=[
            pltpu.VMEM((8, 8, 64, 128), F32),
            pltpu.VMEM((640, 1280), BF16),
            pltpu.VMEM((640, 1280), BF16),
            pltpu.VMEM((16, 64, KC[2]), BF16),
            pltpu.VMEM((16, 64, KC[1]), BF16),
            pltpu.VMEM((16, 64, KC[0]), BF16),
            pltpu.VMEM((8, 128, 512), BF16),
            pltpu.VMEM((8, 128, 640), BF16),
            pltpu.VMEM((8, 128, 640), BF16),
            pltpu.VMEM((2, 8, 640, 128), F32),
            pltpu.VMEM((2, 2, 8, 64, 1280), F32),
            pltpu.VMEM((2, 8, 64, 1280), F32),
            pltpu.VMEM((2, 7, 64, 1280), I16),
            pltpu.VMEM((2, 7, 64, 1280), I16),
            pltpu.VMEM((2, 7, 8, 128), F32),
            pltpu.VMEM((2, 7, 8, 128), F32),
            pltpu.VMEM((2, 7, 640, 128), I16),
            pltpu.VMEM((2, 7, 640, 128), I16),
            pltpu.VMEM((2, 7, 8, 128), F32),
            pltpu.VMEM((2, 7, 8, 128), F32),
            pltpu.VMEM((2, 8, 64, 128), F32),
            pltpu.VMEM((2, 7, 64, 128), F32),
            pltpu.VMEM((3, 640, 128), F32),
            pltpu.VMEM((3, 64, 1280), F32),
            pltpu.VMEM((3, 64, 128), F32),
            pltpu.VMEM((64, 1280), BF16),
            pltpu.VMEM((64, 1280), BF16),
            sem(200),
            sem(200),
            sem(100),
        ],
        compiler_params=pltpu.CompilerParams(
            collective_id=0, has_side_effects=True, vmem_limit_bytes=64000 * 1024),
    )(pattern, region, lin, uin, diag_inv)


def solution(mesh):
    split_mesh = Mesh(mesh.devices.reshape(2, 4, 4, 2, 2), ROW + COL)
    in_specs = (
        P(None, COL, None, ROW),
        P(None, COL, None, ROW),
        P(None, None, COL, ROW),
        P(None, COL, ROW),
        P(),
    )
    out_specs = P(None, COL, None, ROW)
    return jax.shard_map(
        per_device, mesh=split_mesh, in_specs=in_specs, out_specs=out_specs, check_vma=False
    )
```

time: 195 us -> 153 us (0.78); the launches traced: 193 us -> 153 us
  Pallas kernels: 177 us -> 142 us
  local copies, waits for them, and re-layouts: 13.5 us -> 11.1 us
    pallas_call x1, Pallas kernels: 177 us -> 142 us  [per_device(): pl.pallas_call(kernel, name='selinv', out_shape=jax.ShapeDtypeStruct((NSE...]
    slice x4 -> x1, local copies, waits for them, and re-layouts: 3.7 us -> 1.06 us  [per_device(): uin = u_panels[:, 1:].transpose(0, 3, 1, 2).reshape(3, 128, 640)]
where the time goes in v2:
time: 153 us
  Pallas kernels  142 us (93%)
  local copies, waits for them, and re-layouts  11.1 us (7%)
    pallas_call x1, Pallas kernels, per_device(): pl.pallas_call(kernel, name='selinv', out_shape=jax.ShapeDtypeStruct((NSE...  142 us
    pallas_call x1, local copies, waits for them, and re-layouts, per_device(): pl.pallas_call(kernel, name='selinv', out_shape=jax.ShapeDtypeStruct((NSE...  5.76 us

profile of v2, /device:TPU:0, one launch (start us, length us, event | category | flops | bytes accessed | tf_op | source)
XLA Modules:
  0.0 153.2 jit_solution(14091333831935673001)
XLA Ops:
  0.0 1.4 copy.11.pattern
  1.4 1.9 %copy_bitcast_fusion.lin = bf16[3,64,1280]{2,1,0:T(8,128)(2,1)} fusion(bf16[3,64,11,128]{3,1,2,0:T(8,128)(2,1)} %param.6), kind=kLoop, calls=%fused_computation | loop fusion | bytes 983040 | tf_op jit(solution)/shard_map/reshape | solution.py:448
  3.3 1.1 slice.7
  4.3 1.0 copy.12.uin
  5.3 142.0 %selinv.1 = f32[11,64,11,128]{3,2,1,0:T(8,128)} custom-call(s32[3,11,8]{2,1,0:T(8,128)} %copy.11.pattern, f32[8,64,8,128]{3,2,1,0:T(8,128)} %reg.1, bf16[3,64,1280]{2,1,0:T(8,128)(2,1)} %copy_bitcast_fusion.lin, bf16[3,128,640]{2,1,0:T(8,128)(2,1)} %copy.12.uin, f32[3,64,128]{2,1,0:T(8,128)} %diag.1), custom_call_target="tpu_custom_call" | custom-call | tf_op jit(solution)/shard_map/selinv/pallas_call | solution.py:454
  147.4 5.8 %copy.13 = f32[11,64,11,128]{3,1,2,0:T(8,128)} copy(f32[11,64,11,128]{3,2,1,0:T(8,128)} %selinv.1) | data formatting | bytes 7929856 | tf_op jit(solution)/shard_map/selinv/pallas_call | solution.py:454

commit v3 on v0

v3 whole, which is shorter than its diff:
```python
import jax
import jax.numpy as jnp
from jax import lax
from jax.experimental import pallas as pl
from jax.experimental.pallas import tpu as pltpu
from jax.sharding import Mesh
from jax.sharding import PartitionSpec as P

F32 = jnp.float32
BF16 = jnp.bfloat16
I16 = jnp.int16
NSEG = 11
ROW = ("yh", "z")
COL = ("x", "yl", "core")
KC = {2: 1024, 1: 1152, 0: 1280}
U0 = {2: 128, 1: 0, 0: 0}
BUF = {2: 0, 1: 1, 0: 0}
PARTS = {"A": (2, 6), "B": (6, 10)}
TOP = 32700.0
PLAN = (
    "gu2 gl2 gl1 gu1",
    "S2 gu0 gl0 gu2",
    "gu2 H20 gl2 gl2",
    "k2 h20 k2 gl1",
    "gl1 gl2 gu2 H21",
    "H22 k2 h21 gu1",
    "gu1 h22 gu0 gu0",
    "gu2 gu2 H23 r2A",
    "gl1 r2B gl2 gl0",
    "gl0 gu1 r2A r2B",
    "gl2 h23 c2B c2A",
    "gl1 gl1 h11 gu0",
    "gu1 gu1 h10 r2A",
    "H11 H10 c2B r2B",
    "gl0 c2A r2A gu0",
    "gu0 r2B c2B r2A",
    "X1A r1A r2A c2A",
    "gl0 m2A r2B X1B",
    "r1B m2B c2B d2",
    "r1A x1B c1B r1B",
    "c2A x1A T1 t1",
    "r1A c1B d2 u1",
    "r1T c1A r1B r2B",
    "H01 H00 r1A c1B",
    "r1T gl0 c1A h01",
    "r1B h00 r1A r1A",
    "X0A r0A c1A c1T",
    "m1A c1B x0B c0B",
    "r0A r1T m1T r1B",
    "m1B d1 X0B r0B",
    "c1A x0A r0A r1T",
    "c1T T0 r0B c0A",
    "t0 r0A d1 u0",
    "c0T r1B c0B r0T",
    "r0B c0A r0T r0A",
    "r0A m0A r0B c0T",
    "c0B c0A r0T r0T",
    "r0B r0B m0B m0T",
    "d0 c0B c0A d0",
)
MESH = pl.DeviceIdType.MESH


def nt(a, b):
    return lax.dot_general(a, b, (((1,), (1,)), ((), ())), preferred_element_type=F32)


def nn(a, b):
    return lax.dot_general(a, b, (((1,), (0,)), ((), ())), preferred_element_type=F32)


def nt2(hi, lo, w):
    n = hi.shape[0]
    if hi.shape[1] <= 128:
        return nt(jnp.concatenate([hi, lo], axis=1), jnp.concatenate([w, w], axis=1))
    both = nt(jnp.concatenate([hi, lo], axis=0), w)
    return both[:n] + both[n:]


def nn2(w, hi, lo):
    n = hi.shape[1]
    if hi.shape[0] <= 128:
        return nn(jnp.concatenate([w, w], axis=1), jnp.concatenate([hi, lo], axis=0))
    if n <= 128:
        both = nn(w, jnp.concatenate([hi, lo], axis=1))
        return both[:, :n] + both[:, n:]
    return nn(w, hi) + nn(w, lo)


def split(v):
    hi = v.astype(BF16)
    return hi, (v - hi.astype(F32)).astype(BF16)


def pack(ref, v):
    v = v.reshape(-1, 8, 128)
    top = jnp.maximum(jnp.max(jnp.abs(v), axis=0), 1e-30)
    unit = jnp.ceil(jnp.log2(top * (1.0 / TOP)))
    ref[0:16, :] = jnp.concatenate([unit, unit], axis=0).astype(jnp.int32).astype(I16)
    q = jnp.round(v * jnp.exp2(-unit)).reshape(-1, 128)
    ref[16 : 16 + q.shape[0], :] = q.astype(jnp.int32).astype(I16)


def unpack(ref, tiles):
    unit = jnp.exp2(ref[0:16, :].astype(F32)[0:8])
    v = ref[16 : 16 + 64 * tiles, :].astype(F32)
    return (v.reshape(-1, 8, 128) * unit).reshape(tiles, 64, 128)


class Sems:
    def __init__(self, ref):
        self.ref, self.used = ref, 0

    def take(self):
        self.used += 1
        return self.ref.at[self.used - 1]


def kernel(pattern, reg, lin, uin, diag, out, a32, kh, kl, ls2, ls1, ls0, us2, us1, us0, cp, rp, rcl,
           rq_out, rq_in, cq_out, cq_in, dq_out, dq_in, tq_out, tq_in, vq_out, vq_in, dp, cf, rf, df, rh, rl, dkh, dkl,
           send_sem, recv_sem, out_sem):
    ls = {2: ls2, 1: ls1, 0: ls0}
    us = {2: us2, 1: us1, 0: us0}
    yh, z = lax.axis_index("yh"), lax.axis_index("z")
    x, yl, core = lax.axis_index("x"), lax.axis_index("yl"), lax.axis_index("core")
    sends, recvs, outs = Sems(send_sem), Sems(recv_sem), Sems(out_sem)
    out_copies = []

    def mask_row(s, i):
        return pattern[s, i + 1, x * 2 + yl].astype(F32)

    def mask_col(s, i):
        return pattern[s, i + 1, yh * 4 + z].astype(F32)

    def remote(src, dst, where):
        copy = pltpu.make_async_remote_copy(
            src_ref=src, dst_ref=dst, send_sem=sends.take(), recv_sem=recvs.take(),
            device_id=where, device_id_type=MESH)
        copy.start()
        return copy

    def to_out(src, dst):
        copy = pltpu.make_async_copy(src, dst, outs.take())
        copy.start()
        out_copies.append(copy)

    def ring(axis, here):
        places = [lax.rem(here + d, 4) for d in (1, 3, 2)]
        return (*places, {axis: places[0]}, {axis: places[1]})

    offsets = [(a, d) for a in range(2) for d in range(4) if (a, d) != (0, 0)]
    row_peers = [(lax.rem(yh + a, 2), lax.rem(z + d, 4)) for a, d in offsets]
    col_peers = [(lax.rem(yl + a, 2), lax.rem(x + d, 4)) for a, d in offsets]
    with jax.named_scope("signal"):
        barrier = pltpu.get_barrier_semaphore()
        peers = [{"core": 1 - core}]
        peers += [{"yh": a, "z": d} for a, d in row_peers]
        peers += [{"yl": a, "x": d} for a, d in col_peers]
        for peer in peers:
            pl.semaphore_signal(barrier, inc=1, device_id=peer, device_id_type=MESH)
    loads = [pltpu.make_async_copy(reg.at[:, :, b, :], a32.at[b], outs.take()) for b in range(8)]
    for copy in loads:
        copy.start()
    with jax.named_scope("own"):
        lane = lax.broadcasted_iota(jnp.int32, (128, 128), 1)
        for s in (2, 1, 0):
            for i in range(s, 10):
                v = lin[s, :, 128 * i : 128 * (i + 1)].astype(F32) * mask_col(s, i)
                ls[s][(x * 2 + yl) * 2 + core, :, 128 * (i - s) : 128 * (i - s + 1)] = v.astype(BF16)
            for i in range(U0[s] // 128, 5):
                m = jnp.where(lane < 64, mask_row(s, 2 * i), mask_row(s, 2 * i + 1))
                v = uin[s, :, 128 * i : 128 * (i + 1)].astype(F32) * m
                us[s][z * 2 + yh, :, 128 * i - U0[s] : 128 * (i + 1) - U0[s]] = v.astype(BF16)
    with jax.named_scope("barrier"):
        pl.semaphore_wait(barrier, len(peers))

    class Gather:
        def __init__(self, slab, axis, here, pair_axis, pair, to_core):
            self.args = (slab, axis, here, pair_axis, pair, to_core)
            self.started, self.crossed = [], []
            self.steps = self.run()

        def go(self, h, q, where):
            ref = self.args[0](h, q)
            copy = remote(ref, ref, where)
            self.started.append(copy)
            return copy

        def cross(self, h, q):
            if self.args[5]:
                self.crossed.append(self.go(h, q, {"core": 1 - core}))

        def wait_cross(self, count):
            for _ in range(count):
                self.crossed.pop(0).wait_recv()

        def run(self):
            _, axis, here, pair_axis, pair, _ = self.args
            hp, hm, h2, up, down = ring(axis, here)
            oq = 1 - pair
            m_pair = self.go(here, pair, {pair_axis: oq})
            m_op = self.go(here, pair, up)
            m_om = self.go(here, pair, down)
            self.cross(here, pair)
            yield
            m_pair.wait_recv()
            m_tp = self.go(here, oq, up)
            m_tm = self.go(here, oq, down)
            self.cross(here, oq)
            yield
            m_op.wait_recv()
            m_rp = self.go(hm, pair, up)
            self.cross(hm, pair)
            m_om.wait_recv()
            self.cross(hp, pair)
            yield
            m_tm.wait_recv()
            m_rm = self.go(hp, oq, down)
            self.cross(hp, oq)
            m_tp.wait_recv()
            self.cross(hm, oq)
            yield
            m_rp.wait_recv()
            self.cross(h2, pair)
            m_rm.wait_recv()
            self.cross(h2, oq)
            yield
            self.wait_cross(len(self.crossed))
            for copy in self.started:
                copy.wait_send()
            yield

    def gather_l(s):
        slab = ls[s]
        return Gather(lambda h, q: slab.at[(h * 2 + q) * 2 + core], "x", x, "yl", yl, True)

    def gather_u(s):
        slab = us[s]
        return Gather(lambda h, q: slab.at[h * 2 + q], "z", z, "yh", yh, False)

    def reduce_ring(val, q_out, q_in, tiles, axis, here, pair_axis, pair, keep, finish):
        hp, hm, h2, up, down = ring(axis, here)
        oq = 1 - pair
        started = []
        size = slice(0, 16 + 64 * tiles)

        def send(k, v, where):
            pack(q_out.at[k], v)
            copy = remote(q_out.at[k, size, :], q_in.at[k, size, :], where)
            started.append(copy)
            return copy

        def got(k):
            return unpack(q_in.at[k], tiles)

        m_rp = send(0, val(h2, 0), up)
        m_rm = send(1, val(h2, 1), down)
        m_ep = send(3, val(hp, 1), up)
        m_em = send(4, val(hm, 0), down)
        yield
        m_rp.wait_recv()
        m_fp = send(2, val(hp, 0) + got(0), up)
        m_rm.wait_recv()
        m_fm = send(5, val(hm, 1) + got(1), down)
        yield
        for copy in (m_ep, m_em, m_fp, m_fm):
            copy.wait_recv()
        m_y = send(6, val(here, oq) + got(2 + oq) + got(4 + oq), {pair_axis: oq})
        keep(val(here, pair) + got(2 + pair) + got(4 + pair))
        yield
        m_y.wait_recv()
        finish(got(6))
        for copy in started:
            copy.wait_send()
        yield

    def reduce_direct(val, q_out, q_in, tiles, places, finish):
        started = []
        size = slice(0, 16 + 64 * tiles)
        for k, (where, place) in enumerate(places):
            pack(q_out.at[k], val(place))
            started.append(remote(q_out.at[k, size, :], q_in.at[k, size, :], where))
        yield
        total = None
        for k, copy in enumerate(started):
            copy.wait_recv()
            v = unpack(q_in.at[k], tiles)
            total = v if total is None else total + v
        finish(total)
        for copy in started:
            copy.wait_send()
        yield

    row_places = [({"yh": a, "z": d}, a * 4 + d) for a, d in row_peers]
    col_places = [({"yl": a, "x": d}, d * 2 + a) for a, d in col_peers]

    def keep_row(s, i, v):
        rf[s, i] = v
        hi, lo = split(v)
        at = slice(128 * i, 128 * (i + 1))
        rh[:, at] = hi
        rl[:, at] = lo
        if s > 0:
            kh[64 * (s - 1) : 64 * s, at] = hi
            kl[64 * (s - 1) : 64 * s, at] = lo
        to_out(rf.at[s, i], out.at[s, :, i + 1, :])

    def keep_col(s, i, v):
        cf[s, i] = v
        if s > 0:
            hi, lo = split(v)
            kh[64 * i : 64 * (i + 1), 128 * (s - 1) : 128 * s] = hi
            kl[64 * i : 64 * (i + 1), 128 * (s - 1) : 128 * s] = lo

    def rows_part(s, part):
        b = BUF[s]
        lo, hi = PARTS.get(part, (s, 2))
        over = remote(rp.at[b, 1 - core, :, lo:hi], rcl.at[b, :, lo:hi], {"core": 1 - core})
        yield
        over.wait_recv()

        def val(place):
            return rp[b, core, place, lo:hi] + rcl[b, place, lo:hi]

        def keep(v):
            rf[s, lo:hi] = v

        def finish(last):
            for i in range(lo, hi):
                keep_row(s, i, -mask_col(s, i) * (rf[s, i] + last[i - lo]))

        if part == "T":
            keep(val(x * 2 + yl))
            yield from reduce_direct(val, tq_out.at[b], tq_in.at[b], hi - lo, col_places, finish)
        else:
            p = "AB".index(part)
            yield from reduce_ring(lambda h, q: val(h * 2 + q), rq_out.at[b, p], rq_in.at[b, p], hi - lo,
                                   "x", x, "yl", yl, keep, finish)
        over.wait_send()
        yield

    def cols_part(s, part):
        b = BUF[s]
        lo, hi = PARTS.get(part, (s, 2))

        def val(place):
            return cp[b, place, lo:hi]

        def keep(v):
            cf[s, lo:hi] = v

        def finish(last):
            for i in range(lo, hi):
                keep_col(s, i, -mask_row(s, i) * (cf[s, i] + last[i - lo]))
            to_out(cf.at[s, lo:hi], out.at[lo + 1 : hi + 1, :, s, :])

        if part == "T":
            keep(val(yh * 4 + z))
            yield from reduce_direct(val, vq_out.at[b], vq_in.at[b], hi - lo, row_places, finish)
        else:
            p = "AB".index(part)
            yield from reduce_ring(lambda h, q: val(q * 4 + h), cq_out.at[b, p], cq_in.at[b, p], hi - lo,
                                   "z", z, "yh", yh, keep, finish)

    def diag_terms(s, part):
        b = BUF[s]
        lo, hi = PARTS.get(part, (s, 2))

        @pl.loop(0, 4)
        def _(t):
            w = ls[s][pl.ds(4 * t, 4), :, 128 * (lo - s) : 128 * (hi - s)].reshape(256, 128 * (hi - lo))
            at = slice(128 * lo, 128 * hi)
            acc = nt2(rh[:, at], rl[:, at], w)
            for q in range(2):
                if part == "A":
                    dp[b, 2 * t + q] = acc[:, 128 * q : 128 * (q + 1)]
                else:
                    dp[b, 2 * t + q] += acc[:, 128 * q : 128 * (q + 1)]

    def reduce_diag(s):
        b = BUF[s]

        def finish(total):
            v = diag[s] - dp[b, yh * 4 + z] - total[0]
            df[s] = v
            if s > 0:
                at, cols = slice(64 * (s - 1), 64 * s), slice(128 * (s - 1), 128 * s)
                for k, dk, part in zip((kh, kl), (dkh, dkl), split(v)):
                    k[at, cols] = part
                    dk[...] = jnp.zeros((128, 128), BF16)
                    dk[at, :] = part
            to_out(df.at[s], out.at[s, :, s, :])

        yield from reduce_direct(lambda place: dp[b, place], dq_out.at[b], dq_in.at[b], 1, row_places, finish)

    def r_block(s, t, lo, hi, add, mul):
        b = BUF[s]
        acc = mul(us[s][pl.ds(2 * t, 2), :, :].reshape(256, 640 - U0[s]))
        for q in range(4):
            for i in range(lo, hi):
                v = acc[64 * q : 64 * (q + 1), 128 * (i - lo) : 128 * (i - lo + 1)]
                if add:
                    rp[b, q % 2, t + 4 * (q // 2), i] += v
                else:
                    rp[b, q % 2, t + 4 * (q // 2), i] = v

    def c_block(s, t, lo, hi, add, mul):
        b = BUF[s]
        acc = mul(ls[s][pl.ds(4 * t, 4), :, :].reshape(256, KC[s]))
        for q in range(2):
            for i in range(lo, hi):
                v = acc[64 * (i - lo) : 64 * (i - lo + 1), 128 * q : 128 * (q + 1)]
                if add:
                    cp[b, 2 * t + q, i] += v
                else:
                    cp[b, 2 * t + q, i] = v

    def heavy_c(s, t):
        def mul(w):
            w = w[:, 256 - 128 * s :]
            return nt2(kh[128:640, 256:1280], kl[128:640, 256:1280], w)

        c_block(s, t, 2, 10, False, mul)

    def heavy_r(s, t):
        def mul(w):
            w = w[:, 128 - U0[s] :]
            return nn(w, kh[128:640, 256:1280]) + nn(w, kl[128:640, 256:1280])

        r_block(s, t, 2, 10, False, mul)

    def extra_r(s, part):
        lo, hi = PARTS[part]
        at = slice(128 * lo, 128 * hi)

        @pl.loop(0, 4)
        def _(t):
            r_block(s, t, lo, hi, True, lambda w: nn2(w[:, 0:128], kh[0:128, at], kl[0:128, at]))

    def extra_c(s, part):
        lo, hi = PARTS[part]
        at, mid = slice(64 * lo, 64 * hi), slice(128 * s, 256)

        @pl.loop(0, 4)
        def _(t):
            c_block(s, t, lo, hi, True, lambda w: nt2(kh[at, mid], kl[at, mid], w[:, 0 : 256 - 128 * s]))


    def tail_r(s):
        at = slice(128 * s, 256)

        @pl.loop(0, 4)
        def _(t):
            r_block(s, t, s, 2, False, lambda w: nn2(w, kh[0:640, at], kl[0:640, at]))

    def tail_c(s):
        at, cols = slice(64 * s, 128), slice(128 * s, 1280)

        @pl.loop(0, 4)
        def _(t):
            c_block(s, t, s, 2, False, lambda w: nt2(kh[at, cols], kl[at, cols], w))

    def tail_diag(s):
        @pl.loop(0, 4)
        def _(t):
            at = slice(64 * s, 64 * (s + 1))
            r_block(s, t, s, s + 1, True, lambda w: nn2(w[:, 0:128], dkh[...], dkl[...]))
            c_block(s, t, s, s + 1, True, lambda w: nt2(dkh[at, :], dkl[at, :], w[:, 0:128]))

    gl = {s: gather_l(s) for s in (2, 1, 0)}
    gu = {s: gather_u(s) for s in (2, 1, 0)}

    def run(name, f, *args):
        with jax.named_scope(name):
            f(*args)

    def split_region():
        for b in range(8):
            loads[b].wait()
            to_out(a32.at[b], out.at[3:11, :, 3 + b, :])
            hi, lo = split(a32[b].reshape(512, 128))
            kh[128:640, (b + 2) * 128 : (b + 3) * 128] = hi
            kl[128:640, (b + 2) * 128 : (b + 3) * 128] = lo
        for ref in (kh, kl):
            ref[0:128, :] = jnp.zeros((128, 1280), BF16)
            ref[128:640, 0:256] = jnp.zeros((512, 256), BF16)

    places = {}
    for f, axis, here in ((heavy_r, "z", z), (heavy_c, "x", x)):
        up, down, far, *_ = ring(axis, here)
        places[f] = (here, up, down, far)

    def heavy(f, s, piece):
        if s == 2:
            f(s, places[f][piece])
        else:
            pl.loop(2 * piece, 2 * piece + 2)(lambda t: f(s, t))

    R = {(s, p): rows_part(s, p) for s in (2, 1, 0) for p in "ABT"}
    C = {(s, p): cols_part(s, p) for s in (2, 1, 0) for p in "ABT"}
    D = {s: reduce_diag(s) for s in (2, 1, 0)}
    actions = {
        "gl": lambda s, p: next(gl[s].steps),
        "gu": lambda s, p: next(gu[s].steps),
        "k": lambda s, p: gl[s].wait_cross(2),
        "S": lambda s, p: split_region(),
        "H": lambda s, p: heavy(heavy_r, s, int(p)),
        "h": lambda s, p: heavy(heavy_c, s, int(p)),
        "r": lambda s, p: next(R[s, p]),
        "c": lambda s, p: next(C[s, p]),
        "d": lambda s, p: next(D[s]),
        "X": extra_r,
        "x": extra_c,
        "m": diag_terms,
        "T": lambda s, p: tail_r(s),
        "t": lambda s, p: tail_c(s),
        "u": lambda s, p: tail_diag(s),
    }
    for name in " ".join(PLAN).split():
        kind = name[:2] if name[0] == "g" else name[0]
        rest = name[len(kind) :]
        run(name, actions[kind], int(rest[0]), rest[1:])
    for copy in out_copies:
        copy.wait()


def per_device(region, l_panels, u_panels, diag_inv, pattern):
    lin = l_panels[:, :, 1:, :].reshape(3, 64, 1280)
    uin = u_panels[:, 1:].transpose(0, 3, 1, 2).reshape(3, 128, 640)
    smem = pl.BlockSpec(memory_space=pltpu.SMEM)
    vmem = pl.BlockSpec(memory_space=pltpu.VMEM)
    hbm = pl.BlockSpec(memory_space=pl.ANY)
    sem = lambda n: pltpu.SemaphoreType.DMA((n,))
    return pl.pallas_call(
        kernel,
        name="selinv",
        out_shape=jax.ShapeDtypeStruct((NSEG, 64, NSEG, 128), F32),
        in_specs=[smem, hbm, vmem, vmem, vmem],
        out_specs=hbm,
        scratch_shapes=[
            pltpu.VMEM((8, 8, 64, 128), F32),
            pltpu.VMEM((640, 1280), BF16),
            pltpu.VMEM((640, 1280), BF16),
            pltpu.VMEM((16, 64, KC[2]), BF16),
            pltpu.VMEM((16, 64, KC[1]), BF16),
            pltpu.VMEM((16, 64, KC[0]), BF16),
            pltpu.VMEM((8, 128, 512), BF16),
            pltpu.VMEM((8, 128, 640), BF16),
            pltpu.VMEM((8, 128, 640), BF16),
            pltpu.VMEM((2, 8, 10, 64, 128), F32),
            pltpu.VMEM((2, 2, 8, 10, 64, 128), F32),
            pltpu.VMEM((2, 8, 10, 64, 128), F32),
            pltpu.VMEM((2, 2, 7, 272, 128), I16),
            pltpu.VMEM((2, 2, 7, 272, 128), I16),
            pltpu.VMEM((2, 2, 7, 272, 128), I16),
            pltpu.VMEM((2, 2, 7, 272, 128), I16),
            pltpu.VMEM((2, 7, 80, 128), I16),
            pltpu.VMEM((2, 7, 80, 128), I16),
            pltpu.VMEM((2, 7, 144, 128), I16),
            pltpu.VMEM((2, 7, 144, 128), I16),
            pltpu.VMEM((2, 7, 144, 128), I16),
            pltpu.VMEM((2, 7, 144, 128), I16),
            pltpu.VMEM((2, 8, 64, 128), F32),
            pltpu.VMEM((3, 10, 64, 128), F32),
            pltpu.VMEM((3, 10, 64, 128), F32),
            pltpu.VMEM((3, 64, 128), F32),
            pltpu.VMEM((64, 1280), BF16),
            pltpu.VMEM((64, 1280), BF16),
            pltpu.VMEM((128, 128), BF16),
            pltpu.VMEM((128, 128), BF16),
            sem(260),
            sem(260),
            sem(100),
        ],
        compiler_params=pltpu.CompilerParams(
            collective_id=0, has_side_effects=True, vmem_limit_bytes=64000 * 1024),
    )(pattern, region, lin, uin, diag_inv)


def solution(mesh):
    split_mesh = Mesh(mesh.devices.reshape(2, 4, 4, 2, 2), ROW + COL)
    in_specs = (
        P(None, COL, None, ROW),
        P(None, COL, None, ROW),
        P(None, None, COL, ROW),
        P(None, COL, ROW),
        P(),
    )
    out_specs = P(None, COL, None, ROW)
    return jax.shard_map(
        per_device, mesh=split_mesh, in_specs=in_specs, out_specs=out_specs, check_vma=False
    )
```

time: 454 us -> 121 us (0.27)
  waiting for transfers between devices: 198 us -> 0 us
  Pallas kernels: 0 us -> 110 us
  blocking collectives: 79.6 us -> 0 us
  matrix products: 54.8 us -> 0 us
  starting transfers between devices: 39.8 us -> 0 us
  local copies, waits for them, and re-layouts: 38.5 us -> 11.1 us
  other arithmetic: 25.3 us -> 0 us
  between operations: 15.4 us -> 0.01 us
    all_to_all x8 -> x0, waiting for transfers between devices: 157 us -> none  [the longest x6 121 us: summed_on_arrival(): lax.all_to_all(tiles, axis, split_axis=0, concat_axis=0, tiled=True)]
    pallas_call x0 -> x1, Pallas kernels: none -> 110 us  [per_device(): pl.pallas_call(kernel, name='selinv', out_shape=jax.ShapeDtypeStruct((NSE...]
    all_gather x3 -> x0, blocking collectives: 57.9 us -> none  [stacked_from(): tiles = lax.all_gather(tiles, axes[k])]
    dot_general x9 -> x0, matrix products: 54.8 us -> none  [the longest x3 26.6 us: per_device(): jnp.einsum('akw,akbj->wbj', upper_full, known, precision=lax.Precision.HI...]
    all_to_all x8 -> x0, starting transfers between devices: 39.1 us -> none  [the longest x6 31.2 us: summed_on_arrival(): lax.all_to_all(tiles, axis, split_axis=0, concat_axis=0, tiled=True)]
    all_gather x6 -> x0, waiting for transfers between devices: 23 us -> none  [stacked_from(): tiles = lax.all_gather(tiles, axes[k])]
    all_to_all x1 -> x0, blocking collectives: 21.7 us -> none  [from_everyone(): return lax.all_to_all(copies, axis, split_axis=0, concat_axis=0, tiled=True)]
    reduce_scatter x3 -> x0, waiting for transfers between devices: 17.1 us -> none  [per_device(): row_sum = lax.psum_scatter(row_terms, COL, scatter_dimension=0, tiled=True)]
  transfers between devices with their start and end apart: 17 -> 0, of which waited for: 10 -> 0; matrix products, arithmetic and copies ran while one was open for 24% -> 0% of each run, Pallas kernels for 0% -> 0%
where the time goes in v3:
time: 121 us
  Pallas kernels  110 us (91%)
  local copies, waits for them, and re-layouts  11.1 us (9%)
    pallas_call x1, Pallas kernels, per_device(): pl.pallas_call(kernel, name='selinv', out_shape=jax.ShapeDtypeStruct((NSE...  110 us
    pallas_call x1, local copies, waits for them, and re-layouts, per_device(): pl.pallas_call(kernel, name='selinv', out_shape=jax.ShapeDtypeStruct((NSE...  5.76 us

profile of v3, /device:TPU:0, one launch (start us, length us, event | category | flops | bytes accessed | tf_op | source)
XLA Modules:
  0.0 120.8 jit_solution(1800551081672335813)
XLA Ops:
  0.0 1.4 %copy.11.pattern = s32[3,11,8]{2,1,0:T(8,128)} copy(s32[3,11,8]{1,2,0:T(8,128)} %param.9) | data formatting | bytes 2112 | tf_op args[4]
  1.4 1.9 %copy_bitcast_fusion.lin = bf16[3,64,1280]{2,1,0:T(8,128)(2,1)} fusion(bf16[3,64,11,128]{3,1,2,0:T(8,128)(2,1)} %param.6), kind=kLoop, calls=%fused_computation | loop fusion | bytes 983040 | tf_op jit(solution)/shard_map/reshape | solution.py:528
  3.3 1.1 slice.7
  4.3 1.0 copy.12.uin
  5.3 109.7 %selinv.1 = f32[11,64,11,128]{3,2,1,0:T(8,128)} custom-call(s32[3,11,8]{2,1,0:T(8,128)} %copy.11.pattern, f32[8,64,8,128]{3,2,1,0:T(8,128)} %reg.1, bf16[3,64,1280]{2,1,0:T(8,128)(2,1)} %copy_bitcast_fusion.lin, bf16[3,128,640]{2,1,0:T(8,128)(2,1)} %copy.12.uin, f32[3,64,128]{2,1,0:T(8,128)} %diag.1), custom_call_target="tpu_custom_call" | custom-call | tf_op jit(solution)/shard_map/selinv/pallas_call | solution.py:534
  115.0 5.8 %copy.13 = f32[11,64,11,128]{3,1,2,0:T(8,128)} copy(f32[11,64,11,128]{3,2,1,0:T(8,128)} %selinv.1) | data formatting | bytes 7929856 | tf_op jit(solution)/shard_map/selinv/pallas_call | solution.py:534

commit v4 on v3

--- a/solution.py
+++ b/solution.py
@@ -17,6 +17,7 @@
 BUF = {2: 0, 1: 1, 0: 0}
 PARTS = {"A": (2, 6), "B": (6, 10)}
 TOP = 32700.0
+SENDS, RECVS, OUTS = 61, 170, 35
 PLAN = (
     "gu2 gl2 gl1 gu1",
     "S2 gu0 gl0 gu2",
@@ -109,9 +110,11 @@
 
 class Sems:
     def __init__(self, ref):
-        self.ref, self.used = ref, 0
+        self.ref, self.used, self.free = ref, 0, []
 
     def take(self):
+        if self.free:
+            return self.free.pop()
         self.used += 1
         return self.ref.at[self.used - 1]
 
@@ -124,20 +127,29 @@
     yh, z = lax.axis_index("yh"), lax.axis_index("z")
     x, yl, core = lax.axis_index("x"), lax.axis_index("yl"), lax.axis_index("core")
     sends, recvs, outs = Sems(send_sem), Sems(recv_sem), Sems(out_sem)
-    out_copies = []
+    out_copies, send_sems, arrivals = [], {}, {}
 
     def mask_row(s, i):
-        return pattern[s, i + 1, x * 2 + yl].astype(F32)
+        return pattern[s, x * 2 + yl, i + 1].astype(F32)
 
     def mask_col(s, i):
-        return pattern[s, i + 1, yh * 4 + z].astype(F32)
-
-    def remote(src, dst, where):
+        return pattern[s, yh * 4 + z, i + 1].astype(F32)
+
+    def remote(src, dst, where, key=None):
+        sem = sends.take()
+        if key is None or key not in arrivals:
+            arrivals[key] = recvs.take()
         copy = pltpu.make_async_remote_copy(
-            src_ref=src, dst_ref=dst, send_sem=sends.take(), recv_sem=recvs.take(),
+            src_ref=src, dst_ref=dst, send_sem=sem, recv_sem=arrivals[key],
             device_id=where, device_id_type=MESH)
         copy.start()
+        send_sems[id(copy)] = (copy, sem)
         return copy
+
+    def sent(*copies):
+        for copy in copies:
+            copy.wait_send()
+            sends.free.append(send_sems.pop(id(copy))[1])
 
     def to_out(src, dst):
         copy = pltpu.make_async_copy(src, dst, outs.take())
@@ -162,15 +174,14 @@
     for copy in loads:
         copy.start()
     with jax.named_scope("own"):
-        lane = lax.broadcasted_iota(jnp.int32, (128, 128), 1)
         for s in (2, 1, 0):
             for i in range(s, 10):
-                v = lin[s, :, 128 * i : 128 * (i + 1)].astype(F32) * mask_col(s, i)
+                v = lin[s, i + 1].astype(F32) * mask_col(s, i)
                 ls[s][(x * 2 + yl) * 2 + core, :, 128 * (i - s) : 128 * (i - s + 1)] = v.astype(BF16)
-            for i in range(U0[s] // 128, 5):
-                m = jnp.where(lane < 64, mask_row(s, 2 * i), mask_row(s, 2 * i + 1))
-                v = uin[s, :, 128 * i : 128 * (i + 1)].astype(F32) * m
-                us[s][z * 2 + yh, :, 128 * i - U0[s] : 128 * (i + 1) - U0[s]] = v.astype(BF16)
+            for i in range(U0[s] // 64, 10, 2):
+                pair = [uin[s, k + 1].astype(F32) * mask_row(s, k) for k in (i, i + 1)]
+                v = jnp.concatenate(pair, axis=0).T
+                us[s][z * 2 + yh, :, 64 * i - U0[s] : 64 * i + 128 - U0[s]] = v.astype(BF16)
     with jax.named_scope("barrier"):
         pl.semaphore_wait(barrier, len(peers))
 
@@ -226,8 +237,7 @@
             self.cross(h2, oq)
             yield
             self.wait_cross(len(self.crossed))
-            for copy in self.started:
-                copy.wait_send()
+            sent(*self.started)
             yield
 
     def gather_l(s):
@@ -238,7 +248,7 @@
         slab = us[s]
         return Gather(lambda h, q: slab.at[h * 2 + q], "z", z, "yh", yh, False)
 
-    def reduce_ring(val, q_out, q_in, tiles, axis, here, pair_axis, pair, keep, finish):
+    def reduce_ring(key, val, q_out, q_in, tiles, axis, here, pair_axis, pair, keep, finish):
         hp, hm, h2, up, down = ring(axis, here)
         oq = 1 - pair
         started = []
@@ -246,7 +256,7 @@
 
         def send(k, v, where):
             pack(q_out.at[k], v)
-            copy = remote(q_out.at[k, size, :], q_in.at[k, size, :], where)
+            copy = remote(q_out.at[k, size, :], q_in.at[k, size, :], where, (*key, k))
             started.append(copy)
             return copy
 
@@ -270,16 +280,15 @@
         yield
         m_y.wait_recv()
         finish(got(6))
-        for copy in started:
-            copy.wait_send()
-        yield
-
-    def reduce_direct(val, q_out, q_in, tiles, places, finish):
+        sent(*started)
+        yield
+
+    def reduce_direct(key, val, q_out, q_in, tiles, places, finish):
         started = []
         size = slice(0, 16 + 64 * tiles)
         for k, (where, place) in enumerate(places):
             pack(q_out.at[k], val(place))
-            started.append(remote(q_out.at[k, size, :], q_in.at[k, size, :], where))
+            started.append(remote(q_out.at[k, size, :], q_in.at[k, size, :], where, (*key, k)))
         yield
         total = None
         for k, copy in enumerate(started):
@@ -287,8 +296,7 @@
             v = unpack(q_in.at[k], tiles)
             total = v if total is None else total + v
         finish(total)
-        for copy in started:
-            copy.wait_send()
+        sent(*started)
         yield
 
     row_places = [({"yh": a, "z": d}, a * 4 + d) for a, d in row_peers]
@@ -303,7 +311,6 @@
         if s > 0:
             kh[64 * (s - 1) : 64 * s, at] = hi
             kl[64 * (s - 1) : 64 * s, at] = lo
-        to_out(rf.at[s, i], out.at[s, :, i + 1, :])
 
     def keep_col(s, i, v):
         cf[s, i] = v
@@ -315,7 +322,8 @@
     def rows_part(s, part):
         b = BUF[s]
         lo, hi = PARTS.get(part, (s, 2))
-        over = remote(rp.at[b, 1 - core, :, lo:hi], rcl.at[b, :, lo:hi], {"core": 1 - core})
+        over = remote(rp.at[b, 1 - core, :, lo:hi], rcl.at[b, :, lo:hi], {"core": 1 - core},
+                      ("over", b, part))
         yield
         over.wait_recv()
 
@@ -328,15 +336,16 @@
         def finish(last):
             for i in range(lo, hi):
                 keep_row(s, i, -mask_col(s, i) * (rf[s, i] + last[i - lo]))
+            to_out(rf.at[s, lo:hi], out.at[s, lo + 1 : hi + 1])
 
         if part == "T":
             keep(val(x * 2 + yl))
-            yield from reduce_direct(val, tq_out.at[b], tq_in.at[b], hi - lo, col_places, finish)
+            yield from reduce_direct(("rT", b), val, tq_out.at[b], tq_in.at[b], hi - lo, col_places, finish)
         else:
             p = "AB".index(part)
-            yield from reduce_ring(lambda h, q: val(h * 2 + q), rq_out.at[b, p], rq_in.at[b, p], hi - lo,
+            yield from reduce_ring(("r", b, p), lambda h, q: val(h * 2 + q), rq_out.at[b, p], rq_in.at[b, p], hi - lo,
                                    "x", x, "yl", yl, keep, finish)
-        over.wait_send()
+        sent(over)
         yield
 
     def cols_part(s, part):
@@ -352,14 +361,14 @@
         def finish(last):
             for i in range(lo, hi):
                 keep_col(s, i, -mask_row(s, i) * (cf[s, i] + last[i - lo]))
-            to_out(cf.at[s, lo:hi], out.at[lo + 1 : hi + 1, :, s, :])
+            to_out(cf.at[s, lo:hi], out.at[lo + 1 : hi + 1, s])
 
         if part == "T":
             keep(val(yh * 4 + z))
-            yield from reduce_direct(val, vq_out.at[b], vq_in.at[b], hi - lo, row_places, finish)
+            yield from reduce_direct(("cT", b), val, vq_out.at[b], vq_in.at[b], hi - lo, row_places, finish)
         else:
             p = "AB".index(part)
-            yield from reduce_ring(lambda h, q: val(q * 4 + h), cq_out.at[b, p], cq_in.at[b, p], hi - lo,
+            yield from reduce_ring(("c", b, p), lambda h, q: val(q * 4 + h), cq_out.at[b, p], cq_in.at[b, p], hi - lo,
                                    "z", z, "yh", yh, keep, finish)
 
     def diag_terms(s, part):
@@ -389,9 +398,9 @@
                     k[at, cols] = part
                     dk[...] = jnp.zeros((128, 128), BF16)
                     dk[at, :] = part
-            to_out(df.at[s], out.at[s, :, s, :])
-
-        yield from reduce_direct(lambda place: dp[b, place], dq_out.at[b], dq_in.at[b], 1, row_places, finish)
+            to_out(df.at[s], out.at[s, s])
+
+        yield from reduce_direct(("d", b), lambda place: dp[b, place], dq_out.at[b], dq_in.at[b], 1, row_places, finish)
 
     def r_block(s, t, lo, hi, add, mul):
         b = BUF[s]
@@ -477,7 +486,7 @@
     def split_region():
         for b in range(8):
             loads[b].wait()
-            to_out(a32.at[b], out.at[3:11, :, 3 + b, :])
+            to_out(a32.at[b], out.at[3:11, 3 + b])
             hi, lo = split(a32[b].reshape(512, 128))
             kh[128:640, (b + 2) * 128 : (b + 3) * 128] = hi
             kl[128:640, (b + 2) * 128 : (b + 3) * 128] = lo
@@ -520,21 +529,22 @@
         kind = name[:2] if name[0] == "g" else name[0]
         rest = name[len(kind) :]
         run(name, actions[kind], int(rest[0]), rest[1:])
-    for copy in out_copies:
-        copy.wait()
+    with jax.named_scope("outs"):
+        for copy in out_copies:
+            copy.wait()
 
 
 def per_device(region, l_panels, u_panels, diag_inv, pattern):
-    lin = l_panels[:, :, 1:, :].reshape(3, 64, 1280)
-    uin = u_panels[:, 1:].transpose(0, 3, 1, 2).reshape(3, 128, 640)
+    lin = l_panels.transpose(0, 2, 1, 3)
+    blocks = pattern.transpose(0, 2, 1)
     smem = pl.BlockSpec(memory_space=pltpu.SMEM)
     vmem = pl.BlockSpec(memory_space=pltpu.VMEM)
     hbm = pl.BlockSpec(memory_space=pl.ANY)
     sem = lambda n: pltpu.SemaphoreType.DMA((n,))
-    return pl.pallas_call(
+    blocks_out = pl.pallas_call(
         kernel,
         name="selinv",
-        out_shape=jax.ShapeDtypeStruct((NSEG, 64, NSEG, 128), F32),
+        out_shape=jax.ShapeDtypeStruct((NSEG, NSEG, 64, 128), F32),
         in_specs=[smem, hbm, vmem, vmem, vmem],
         out_specs=hbm,
         scratch_shapes=[
@@ -568,13 +578,14 @@
             pltpu.VMEM((64, 1280), BF16),
             pltpu.VMEM((128, 128), BF16),
             pltpu.VMEM((128, 128), BF16),
-            sem(260),
-            sem(260),
-            sem(100),
+            sem(SENDS),
+            sem(RECVS),
+            sem(OUTS),
         ],
         compiler_params=pltpu.CompilerParams(
             collective_id=0, has_side_effects=True, vmem_limit_bytes=64000 * 1024),
-    )(pattern, region, lin, uin, diag_inv)
+    )(blocks, region, lin, u_panels, diag_inv)
+    return blocks_out.transpose(0, 2, 1, 3)
 
 
 def solution(mesh):

time: 121 us -> 111 us (0.917)
  local copies, waits for them, and re-layouts: 11.1 us -> 4.6 us
  Pallas kernels: 110 us -> 106 us
    pallas_call x1 -> x0, local copies, waits for them, and re-layouts: 5.76 us -> none  [per_device(): pl.pallas_call(kernel, name='selinv', out_shape=jax.ShapeDtypeStruct((NSE...]
    pallas_call x1, Pallas kernels: 110 us -> 106 us  [per_device(): pl.pallas_call(kernel, name='selinv', out_shape=jax.ShapeDtypeStruct((NSE...]
    unnamed x1, local copies, waits for them, and re-layouts: 1.4 us -> 4.6 us
    reshape x2 -> x0, local copies, waits for them, and re-layouts: 2.87 us -> none  [the longest x1 1.86 us: per_device(): lin = l_panels[:, :, 1:, :].reshape(3, 64, 1280)]
where the time goes in v4:
time: 111 us
  Pallas kernels  106 us (95%)
  local copies, waits for them, and re-layouts  4.6 us (4%)
    pallas_call x1, Pallas kernels, per_device(): pl.pallas_call(kernel, name='selinv', out_shape=jax.ShapeDtypeStruct((NSE...  106 us
    unnamed x1, local copies, waits for them, and re-layouts  4.6 us

profile of v4, /device:TPU:0, one launch (start us, length us, event | category | flops | bytes accessed | tf_op | source)
XLA Modules:
  0.0 110.8 jit_solution(6742354708292846561)
XLA Ops:
  0.0 106.2 %selinv.1 = f32[11,11,64,128]{3,2,1,0:T(8,128)} custom-call(s32[3,8,11]{2,1,0:T(8,128)} %bitcast.5, f32[8,64,8,128]{3,2,1,0:T(8,128)} %reg.1, bf16[3,11,64,128]{3,2,1,0:T(8,128)(2,1)} %bitcast.4, bf16[3,11,64,128]{3,2,1,0:T(8,128)(2,1)} %uin.1, f32[3,64,128]{2,1,0:T(8,128)} %diag.1), custom_call_target="tpu_custom_call" | custom-call | tf_op jit(solution)/shard_map/selinv/pallas_call | solution.py:544
  106.2 4.6 %copy.7 = f32[11,64,11,128]{3,1,2,0:T(8,128)} copy(f32[11,64,11,128]{3,1,2,0:T(8,128)} %bitcast.3) | data formatting | bytes 7929856

commit v5 on v4

--- a/solution.py
+++ b/solution.py
@@ -17,47 +17,47 @@
 BUF = {2: 0, 1: 1, 0: 0}
 PARTS = {"A": (2, 6), "B": (6, 10)}
 TOP = 32700.0
-SENDS, RECVS, OUTS = 61, 170, 35
+SENDS, RECVS, OUTS = 61, 170, 39
 PLAN = (
     "gu2 gl2 gl1 gu1",
-    "S2 gu0 gl0 gu2",
-    "gu2 H20 gl2 gl2",
+    "gu0 gl0 S2 gu2",
+    "H20 gu2 gl2 gl2",
     "k2 h20 k2 gl1",
     "gl1 gl2 gu2 H21",
-    "H22 k2 h21 gu1",
-    "gu1 h22 gu0 gu0",
-    "gu2 gu2 H23 r2A",
-    "gl1 r2B gl2 gl0",
-    "gl0 gu1 r2A r2B",
-    "gl2 h23 c2B c2A",
-    "gl1 gl1 h11 gu0",
-    "gu1 gu1 h10 r2A",
-    "H11 H10 c2B r2B",
-    "gl0 c2A r2A gu0",
-    "gu0 r2B c2B r2A",
-    "X1A r1A r2A c2A",
-    "gl0 m2A r2B X1B",
-    "r1B m2B c2B d2",
-    "r1A x1B c1B r1B",
-    "c2A x1A T1 t1",
-    "r1A c1B d2 u1",
-    "r1T c1A r1B r2B",
-    "H01 H00 r1A c1B",
-    "r1T gl0 c1A h01",
-    "r1B h00 r1A r1A",
-    "X0A r0A c1A c1T",
-    "m1A c1B x0B c0B",
-    "r0A r1T m1T r1B",
-    "m1B d1 X0B r0B",
-    "c1A x0A r0A r1T",
-    "c1T T0 r0B c0A",
-    "t0 r0A d1 u0",
-    "c0T r1B c0B r0T",
-    "r0B c0A r0T r0A",
-    "r0A m0A r0B c0T",
-    "c0B c0A r0T r0T",
-    "r0B r0B m0B m0T",
-    "d0 c0B c0A d0",
+    "gu1 gu1 H22 k2",
+    "h22 h21 gu0 gu0",
+    "gu2 H23 gl1 r2A",
+    "r2B gl2 gl0 gl0",
+    "gu2 gu1 r2A r2B",
+    "gl2 gl1 h23 c2B",
+    "c2A gl1 h11 h10",
+    "gu0 gu1 gu1 H11",
+    "r2A H10 c2B r2B",
+    "gl0 c2A r2A r2B",
+    "gu0 gu0 c2B r2A",
+    "X1A gl0 r2A c2A",
+    "r2B r1A m2A m2B",
+    "gl0 d2 X1B r1A",
+    "r1B c2B x1B c2A",
+    "c1B t1 r1B x1A",
+    "c1A r1A T1 d2",
+    "u1 c1T r1T r1B",
+    "c1B r2B H00 c1A",
+    "r1T h00 r1A H01",
+    "c1T r1B h01 c1A",
+    "c1B r1T r1A r1A",
+    "X0A r0A m1A r1B",
+    "r1B m1B m1T d1",
+    "r0A c1A X0B r0B",
+    "x0A c0A c1B T0",
+    "r0A r0B t0 d1",
+    "u0 c0T c0A x0B",
+    "r0A r0T c0B r1T",
+    "r0B r0T r0B c0T",
+    "c0A r0A r0A m0A",
+    "c0B r0T r0B r0B",
+    "m0T c0B r0T m0B",
+    "d0 c0A c0B d0",
 )
 MESH = pl.DeviceIdType.MESH
 
@@ -119,7 +119,7 @@
         return self.ref.at[self.used - 1]
 
 
-def kernel(pattern, reg, lin, uin, diag, out, a32, kh, kl, ls2, ls1, ls0, us2, us1, us0, cp, rp, rcl,
+def kernel(pattern_in, reg, lin_in, uin_in, diag_in, out, pattern, lin, uin, diag, a32, kh, kl, ls2, ls1, ls0, us2, us1, us0, cp, rp, rcl,
            rq_out, rq_in, cq_out, cq_in, dq_out, dq_in, tq_out, tq_in, vq_out, vq_in, dp, cf, rf, df, rh, rl, dkh, dkl,
            send_sem, recv_sem, out_sem):
     ls = {2: ls2, 1: ls1, 0: ls0}
@@ -170,9 +170,15 @@
         peers += [{"yl": a, "x": d} for a, d in col_peers]
         for peer in peers:
             pl.semaphore_signal(barrier, inc=1, device_id=peer, device_id_type=MESH)
+    inputs = [pltpu.make_async_copy(src, dst, outs.take()) for src, dst in (
+        (pattern_in, pattern), (lin_in, lin), (uin_in, uin), (diag_in, diag))]
+    for copy in inputs:
+        copy.start()
     loads = [pltpu.make_async_copy(reg.at[:, :, b, :], a32.at[b], outs.take()) for b in range(8)]
     for copy in loads:
         copy.start()
+    for copy in inputs:
+        copy.wait()
     with jax.named_scope("own"):
         for s in (2, 1, 0):
             for i in range(s, 10):
@@ -534,20 +540,34 @@
             copy.wait()
 
 
+def pass_on(src, dst, held, in_sem, out_sem):
+    into = [pltpu.make_async_copy(src.at[a], held.at[a], in_sem.at[a]) for a in range(NSEG)]
+    onward = [pltpu.make_async_copy(held.at[a], dst.at[a], out_sem.at[a]) for a in range(NSEG)]
+    for copy in into:
+        copy.start()
+    for first, second in zip(into, onward):
+        first.wait()
+        second.start()
+    for copy in onward:
+        copy.wait()
+
+
 def per_device(region, l_panels, u_panels, diag_inv, pattern):
     lin = l_panels.transpose(0, 2, 1, 3)
     blocks = pattern.transpose(0, 2, 1)
-    smem = pl.BlockSpec(memory_space=pltpu.SMEM)
-    vmem = pl.BlockSpec(memory_space=pltpu.VMEM)
     hbm = pl.BlockSpec(memory_space=pl.ANY)
     sem = lambda n: pltpu.SemaphoreType.DMA((n,))
     blocks_out = pl.pallas_call(
         kernel,
         name="selinv",
         out_shape=jax.ShapeDtypeStruct((NSEG, NSEG, 64, 128), F32),
-        in_specs=[smem, hbm, vmem, vmem, vmem],
+        in_specs=[hbm] * 5,
         out_specs=hbm,
         scratch_shapes=[
+            pltpu.SMEM((3, 8, NSEG), jnp.int32),
+            pltpu.VMEM((3, NSEG, 64, 128), BF16),
+            pltpu.VMEM((3, NSEG, 64, 128), BF16),
+            pltpu.VMEM((3, 64, 128), F32),
             pltpu.VMEM((8, 8, 64, 128), F32),
             pltpu.VMEM((640, 1280), BF16),
             pltpu.VMEM((640, 1280), BF16),
@@ -585,7 +605,16 @@
         compiler_params=pltpu.CompilerParams(
             collective_id=0, has_side_effects=True, vmem_limit_bytes=64000 * 1024),
     )(blocks, region, lin, u_panels, diag_inv)
-    return blocks_out.transpose(0, 2, 1, 3)
+    result = pl.pallas_call(
+        pass_on,
+        name="pass_on",
+        out_shape=jax.ShapeDtypeStruct((NSEG, NSEG, 64, 128), F32),
+        in_specs=[hbm],
+        out_specs=hbm,
+        scratch_shapes=[pltpu.VMEM((NSEG, NSEG, 64, 128), F32), sem(NSEG), sem(NSEG)],
+        compiler_params=pltpu.CompilerParams(vmem_limit_bytes=64000 * 1024),
+    )(blocks_out)
+    return result.transpose(0, 2, 1, 3)
 
 
 def solution(mesh):

time: 111 us -> 107 us (0.964)
  local copies, waits for them, and re-layouts: 4.6 us -> 0 us
    unnamed x1 -> x0, local copies, waits for them, and re-layouts: 4.6 us -> none
    pallas_call x0 -> x1, Pallas kernels: none -> 3.47 us  [per_device(): pl.pallas_call(pass_on, name='pass_on', out_shape=jax.ShapeDtypeStruct((N...]
    pallas_call x1, Pallas kernels: 106 us -> 103 us  [per_device(): pl.pallas_call(kernel, name='selinv', out_shape=jax.ShapeDtypeStruct((NSE...]
where the time goes in v5:
time: 107 us
  Pallas kernels  106 us (99%)
    pallas_call x1, Pallas kernels, per_device(): pl.pallas_call(kernel, name='selinv', out_shape=jax.ShapeDtypeStruct((NSE...  103 us
    pallas_call x1, Pallas kernels, per_device(): pl.pallas_call(pass_on, name='pass_on', out_shape=jax.ShapeDtypeStruct((N...  3.47 us

profile of v5, /device:TPU:0, one launch (start us, length us, event | category | flops | bytes accessed | tf_op | source)
XLA Modules:
  0.0 106.6 jit_solution(3703533963837172668)
XLA Ops:
  0.0 102.9 %selinv.1.src = f32[11,11,64,128]{3,2,1,0:T(8,128)} custom-call(s32[3,8,11]{2,1,0:T(8,128)} %bitcast.4, f32[8,64,8,128]{3,2,1,0:T(8,128)} %reg.1, bf16[3,11,64,128]{3,2,1,0:T(8,128)(2,1)} %bitcast.3, bf16[3,11,64,128]{3,2,1,0:T(8,128)(2,1)} %uin_in.1, f32[3,64,128]{2,1,0:T(8,128)} %diag_in.1), custom_call_target="tpu_custom_call" | custom-call | tf_op jit(solution)/shard_map/selinv/pallas_call | solution.py:560
  102.9 3.5 %pass_on.1 = f32[11,11,64,128]{3,2,1,0:T(8,128)} custom-call(f32[11,11,64,128]{3,2,1,0:T(8,128)} %selinv.1.src), custom_call_target="tpu_custom_call" | custom-call | tf_op jit(solution)/shard_map/pass_on/pallas_call | solution.py:608
